TPU v7x, 128 devices: a whole 4x4x4 slice. The times are simulated.
128 devices in a mesh: aux: 8 (over z, core), orb: 16 (over x, y).
Axes of the slice: x: 4, y: 4, z: 4, core: 2. Of those that a mesh axis runs over, the one named last changes fastest.
Arguments:
- half: bfloat16 [128, 384, 3072], P('aux', 'orb'), may hold values from -1 to 1
- metric: bfloat16 [128, 128], P('aux'), may hold values from -1 to 2
- survive: int32 [8, 16, 24], P('aux', 'orb'), may hold values 0 or 1
Outputs:
- exchange_k: float32 [3072, 3072], P('orb', 'aux')
All inputs are finite; a program needn't handle non-finite values. No bound on the sum of `survive` on one device may be relied on, other than what follows from the above.
Results may differ from a plain program's by a relative error of at most 0.00098.
Values may be sent and summed in bfloat16 or wider, within the bound.
A program may use at most 128 MiB of HBM per device.

v0:
```python
import jax
import jax.numpy as jnp
from jax import lax
from jax.sharding import Mesh
from jax.sharding import PartitionSpec as P

AUX = ("aux_0", "aux_1")


def sum_by_axis(x, axes, dim):
    for axis in axes:
        x = lax.psum_scatter(x, axis, scatter_dimension=dim, tiled=True)
    return x


def shards(half, metric, survive):
    aux_local, occ_local, ao_count = half.shape
    blocks_aux, blocks_occ, blocks_ao = survive.shape
    gate = survive.astype(jnp.bfloat16)
    shaped = half.reshape(
        blocks_aux, aux_local, blocks_occ, occ_local // blocks_occ, blocks_ao, ao_count // blocks_ao
    )
    masked = (shaped * gate[:, None, :, None, :, None]).reshape(aux_local, occ_local, ao_count)
    portion = lax.all_gather(masked, AUX, axis=0, tiled=True)
    fit_total = jnp.dot(
        metric, portion.reshape(portion.shape[0], -1), preferred_element_type=jnp.float32
    )
    fitted = fit_total.astype(jnp.bfloat16).reshape(aux_local, occ_local, ao_count)
    group_width = ao_count // lax.axis_size("orb")
    row_start = lax.axis_index("orb") * group_width
    flat_rows = lax.all_gather(fitted, "orb", axis=1, tiled=True).reshape(-1, ao_count)
    left_rows = lax.dynamic_slice_in_dim(flat_rows, row_start, group_width, 1)
    partial_k = lax.dot_general(
        left_rows, flat_rows, (((0,), (0,)), ((), ())), preferred_element_type=jnp.float32
    )
    return sum_by_axis(partial_k, AUX, 1)


def solution(mesh):
    finer = Mesh(mesh.devices.reshape(4, 2, mesh.shape["orb"]), ("aux_0", "aux_1", "orb"))
    placed = (P(AUX, "orb", None), P(AUX, None), P(AUX, "orb", None))
    return jax.shard_map(
        shards, mesh=finer, in_specs=placed, out_specs=P("orb", AUX), check_vma=False
    )
```

profile of v0, /device:TPU:47, one launch (start us, length us, event | category | flops | bytes accessed | tf_op | source)
XLA Modules:
  0.0 418.4 jit_solution(15447254739541750862)
XLA Ops:
  6.5 0.0 copy-start
  6.5 0.0 all-gather.3.cloned.1.call-start
  6.5 0.7 convert_bitcast_fusion
  7.2 0.1 broadcast_bitcast_fusion
  7.3 3.2 broadcast_multiply_fusion
  10.5 0.0 all-gather.3.cloned.1.call-update
  10.5 0.0 all-gather.5.cloned.1.call-start
  10.6 95.9 %all-gather.3.cloned.1.call-done = bf16[128,24,3072]{2,1,0:T(8,128)(2,1)} async-done(((bf16[16,24,3072]{2,1,0:T(8,128)(2,1)}), bf16[128,24,3072]{2,1,0:T(8,128)(2,1)}) %all-gather.3.cloned.1.call-update) | async-done | bytes 18874384 | tf_op jit(solution)/shard_map/all_gather | solution.py:24
  106.5 17.4 %copy.4 = bf16[16,8,24,3072]{3,1,2,0:T(8,128)(2,1)S(1)} copy(bf16[16,8,24,3072]{3,2,1,0:T(8,128)(2,1)} %bitcast.15) | data formatting | bytes 37748736
  123.9 0.0 copy-done
  123.9 2.7 convolution_convert_fusion
  126.6 2.7 copy.5
  129.3 0.0 all-gather.5.cloned.1.call-update
  129.3 0.0 reduce-scatter.3.cloned.1.call-start
  129.4 217.5 %all-gather.5.cloned.1.call-done = bf16[16,384,3072]{2,1,0:T(8,128)(2,1)} async-done(((bf16[16,24,3072]{2,1,0:T(8,128)(2,1)}), bf16[16,384,3072]{2,1,0:T(8,128)(2,1)}) %all-gather.5.cloned.1.call-update) | async-done | bytes 37748752 | tf_op jit(solution)/shard_map/all_gather | solution.py:31
  346.9 0.0 copy-start.1
  346.9 18.5 %fusion = f32[192,3072]{1,0:T(8,128)} fusion(bf16[6144,3072]{1,0:T(8,128)(2,1)} %bitcast.14, s32[]{:T(128)S(6)} %select_n.3), kind=kOutput, calls=%fused_computation.1 | convolution fusion | flops 7247757312 | bytes 43253764 | tf_op jit(solution)/shard_map/dot_general | solution.py:33
  365.4 0.0 reduce-scatter.3.cloned.1.call-update
  365.4 0.0 reduce-scatter.5.cloned.1.call-start
  365.5 31.9 %reduce-scatter.3.cloned.1.call-done = f32[192,768]{1,0:T(8,128)} async-done(((f32[192,3072]{1,0:T(8,128)}), f32[192,768]{1,0:T(8,128)}) %reduce-scatter.3.cloned.1.call-update) | async-done | bytes 589840 | tf_op jit(solution)/shard_map/reduce_scatter | solution.py:12
  397.3 0.0 reduce-scatter.5.cloned.1.call-update
  397.3 14.5 %reduce-scatter.5.cloned.1.call-done = f32[192,384]{1,0:T(8,128)} async-done(((f32[192,768]{1,0:T(8,128)}), f32[192,384]{1,0:T(8,128)}) %reduce-scatter.5.cloned.1.call-update) | async-done | bytes 294928 | tf_op jit(solution)/shard_map/reduce_scatter | solution.py:12
  411.9 0.0 copy-done.1
Async XLA Ops:
  6.5 117.4 %copy-start = (bf16[16,128]{1,0:T(8,128)(2,1)S(1)}, bf16[16,128]{1,0:T(8,128)(2,1)}, u32[]{:S(2)}) copy-start(bf16[16,128]{1,0:T(8,128)(2,1)} %param.4) | copy-start | bytes 12292
  6.5 99.9 %all-gather.3.cloned.1.call-start = ((), (), s32[]{:S(2)}) async-start(), calls=%async_computation.2 | async-start | bytes 21233664 | tf_op jit(solution)/shard_map/all_gather | solution.py:24
  10.5 336.4 %all-gather.5.cloned.1.call-start = ((), (), s32[]{:S(2)}) async-start(), calls=%async_computation.3 | async-start | bytes 40108032 | tf_op jit(solution)/shard_map/all_gather | solution.py:31
  129.3 268.0 %reduce-scatter.3.cloned.1.call-start = ((), (), s32[]{:S(2)}) async-start(), calls=%async_computation.4 | async-start | bytes 2949120 | tf_op jit(solution)/shard_map/reduce_scatter | solution.py:12
  346.9 64.9 %copy-start.1 = (bf16[16,128]{1,0:T(8,128)(2,1)S(1)}, bf16[16,128]{1,0:T(8,128)(2,1)}, u32[]{:S(2)}) copy-start(bf16[16,128]{1,0:T(8,128)(2,1)} %param.4) | copy-start | bytes 12292
  365.4 46.4 %reduce-scatter.5.cloned.1.call-start = ((), (), s32[]{:S(2)}) async-start(), calls=%async_computation.5 | async-start | bytes 884736 | tf_op jit(solution)/shard_map/reduce_scatter | solution.py:12
Sparse Core Ops, SparseCore 0:
  10.6 95.7 all-gather.2
  129.5 217.4 all-gather.4
  365.5 31.7 reduce-scatter.2
  399.5 12.2 reduce-scatter.4
where the time goes:
time: 420 us; the launch traced here: 418 us
  waiting for transfers between devices  360 us (86%)
  matrix products  21.2 us (5%)
  local copies, waits for them, and re-layouts  20.2 us (5%)
  between operations  13.2 us (3%)
    all_gather x1, waiting for transfers between devices, shards(): lax.all_gather(fitted, 'orb', axis=1, tiled=True).reshape(-1, ao_count)  218 us
    all_gather x1, waiting for transfers between devices, shards(): portion = lax.all_gather(masked, AUX, axis=0, tiled=True)  95.9 us
    reduce_scatter x2, waiting for transfers between devices, sum_by_axis(): x = lax.psum_scatter(x, axis, scatter_dimension=dim, tiled=True)  46.4 us
    unnamed x6, local copies, waits for them, and re-layouts  20.1 us
    dot_general x1, matrix products, shards(): lax.dot_general(left_rows, flat_rows, (((0,), (0,)), ((), ())), preferred...  18.5 us
  transfers between devices with their start and end apart: 4, of which 4 were waited for; matrix products, arithmetic and copies ran while one was open for 0% of the time, Pallas kernels for 0%

commit v1 on v0

v1 whole, which is shorter than its diff:
```python
import jax
import jax.numpy as jnp
import numpy as np
from jax import lax
from jax.experimental import pallas as pl
from jax.experimental.pallas import tpu as pltpu
from jax.sharding import PartitionSpec as P

MESH = pl.DeviceIdType.MESH
CH = 384
NCH = 8
TR = 192
HR = 96
TOP = 32700.0
TINY = 1e-36


def perm_matrix():
    m = np.zeros((CH, CH), np.float32)
    for d in range(8):
        for aux in range(16):
            for i in range(3):
                m[d * 48 + aux * 3 + i, aux * 24 + 3 * d + i] = 1.0
    return m


def kernel(half, mask, kron, perm, out, snd, rcv, rel, m3, fb, ft, dv, cs, csi, rb, rbi,
           s1f, s1n, r1f, r1n, kown, s2f, s2n, r2f, r2n, s3, r3, s4, r4,
           p1s, p1r, rls, rlr, fws, ks, kr, fs, fr, ds_, dr,
           q1fs, q1fr, q1ns, q1nr, q2fs, q2fr, q2ns, q2nr, q3s, q3r, q4s, q4r):
    f32 = jnp.float32
    aux = lax.axis_index("aux")
    orb = lax.axis_index("orb")
    z, c = aux // 2, aux % 2
    x, y = orb // 4, orb % 4
    me1 = x * (1 - c) + y * c
    me2 = y * (1 - c) + x * c
    sib = 2 * z + 1 - c

    def row_of(t, u):
        return t * (4 - 3 * c) + u * (1 + 3 * c)

    def ring1(o):
        return (aux, row_of((me1 + o) % 4, me2))

    def ring2(o):
        return (aux, row_of(me1, (me2 + o) % 4))

    def zdev(o, core):
        return (2 * ((z + o) % 4) + core, orb)

    pr = orb // 2
    mirror = [(2 * aux + h, pr) for h in range(2)]
    has_mirror = aux != pr

    bar = pltpu.get_barrier_semaphore()
    for o in range(1, 8):
        pl.semaphore_signal(bar, inc=1, device_id=((aux + o) % 8, orb), device_id_type=MESH)
    for o in range(1, 4):
        pl.semaphore_signal(bar, inc=1, device_id=ring1(o), device_id_type=MESH)
        pl.semaphore_signal(bar, inc=1, device_id=ring2(o), device_id_type=MESH)

    @pl.when(has_mirror)
    def _():
        for o, a in mirror:
            pl.semaphore_signal(bar, inc=1, device_id=(a, o), device_id_type=MESH)
        pl.semaphore_wait(bar, 15)

    @pl.when(jnp.logical_not(has_mirror))
    def _():
        pl.semaphore_wait(bar, 13)

    def rcopy(src, dst, ss, rs, dev):
        return pltpu.make_async_remote_copy(src_ref=src, dst_ref=dst, send_sem=ss, recv_sem=rs,
                                            device_id=dev, device_id_type=MESH)

    def al48(v):
        return pl.ds(pl.multiple_of(v * 48, 16), 48)

    def al96(v):
        return pl.ds(pl.multiple_of(v * 96, 16), 96)

    def krcopy(o):
        dst = m3.at[al48(aux)]
        return rcopy(kron, dst, ks.at[o], kr.at[o], ((aux + o) % 8, orb))

    for o in range(1, 8):
        krcopy(o).start()
    m3[al48(aux), :] = kron[...]

    step = 1 - 2 * c + 4
    zr = (z + step) % 4
    zf = (z + 4 - (step - 4)) % 4

    def near(q, o, core):
        dst_dev = zdev(o, core)
        rows = 2 * ((z + o) % 4) + core
        return rcopy(snd.at[q, al48(rows)], rcv.at[q, al48(aux)],
                     p1s.at[q, 2 * (o - 1) + core], p1r.at[q, aux], dst_dev)

    def sibling(q):
        return rcopy(snd.at[q, al48(sib)], rcv.at[q, al48(aux)], p1s.at[q, 2], p1r.at[q, aux], (sib, orb))

    def relay(q):
        return rcopy(snd.at[q, al96((z + 2) % 4)], rel.at[q], rls.at[q], rlr.at[q], (2 * zr + c, orb))

    def forward(q, core):
        src_aux = 2 * zf + c
        return rcopy(rel.at[q, pl.ds(48 * core, 48)], rcv.at[q, al48(src_aux)],
                     fws.at[q, core], p1r.at[q, src_aux], (2 * zr + core, orb))

    def arrival(q, a):
        return rcopy(rcv.at[q, al48(a)], rcv.at[q, al48(a)], p1s.at[q, 0], p1r.at[q, a], (sib, orb))

    def cut(q):
        return pl.ds(pl.multiple_of(q * CH, 128), CH)

    @pl.loop(0, NCH)
    def _(q):
        block = half[:, cut(q)] * mask[:, cut(q)]
        snd[q] = jnp.dot(perm[...], block, preferred_element_type=f32).astype(jnp.bfloat16)
        relay(q).start()
        for core in range(2):
            near(q, 1, core).start()
            near(q, 3, core).start()
        sibling(q).start()
        rcv[q, al48(aux), :] = snd[q, al48(aux), :]

    for o in range(1, 8):
        src = (aux + 8 - o) % 8
        rcopy(kron, m3.at[al48(src)], ks.at[o], kr.at[o], (sib, orb)).wait_recv()

    def fcopy(q):
        return rcopy(fb.at[q, pl.ds(0, CH)], fb.at[q, pl.ds(CH, CH)], fs.at[q], fr.at[q], (sib, orb))

    @pl.loop(0, NCH)
    def _(q):
        relay(q).wait_recv()
        for core in range(2):
            forward(q, core).start()

    @pl.loop(0, NCH)
    def _(q):
        for o in range(1, 8):
            arrival(q, (aux + o) % 8).wait_recv()
        fb[q, 0:CH, :] = jnp.dot(m3[...], rcv[q], preferred_element_type=f32).astype(jnp.bfloat16)
        fcopy(q).start()

    @pl.loop(0, NCH)
    def _(q):
        fcopy(q).wait_recv()
        both = fb[q]
        ft[q] = both.T
        wide = both.astype(f32)
        dv[0, pl.ds(q, 1), :] = jnp.sum(wide * wide, axis=0, keepdims=True)

    def tables(first, terms):
        for n, val in enumerate(terms):
            val = jnp.maximum(val, TINY)
            lane = lax.broadcasted_iota(jnp.int32, val.shape, 1)
            inv = lax.rsqrt(val)
            csi[first + n] = inv
            cs[first + n] = val * inv
            for h in range(2):
                part = jnp.where((lane >= TR) == (h == 1), val, TINY)
                top = jnp.broadcast_to(jnp.max(part, axis=1, keepdims=True), val.shape)
                tinv = lax.rsqrt(top)
                rbi[first + n, h] = tinv * TOP
                rb[first + n, h] = top * tinv * (1.0 / TOP)

    def gather(level, dev):
        base = 4 * level
        for o in range(1, 4):
            rcopy(dv.at[base], dv.at[base + 4 - o], ds_.at[base + o], dr.at[base + 4 - o], dev(o)).start()

    def gathered(level, dev):
        base = 4 * level
        for o in range(1, 4):
            rcopy(dv.at[base], dv.at[base + o], ds_.at[base + o], dr.at[base + o], dev(o)).wait_recv()
        return [dv[base + o] for o in range(4)]

    def ring_terms(d):
        return [d[0], d[3], d[1], d[0] + d[3], d[0] + d[1], d[3] + d[2], d[1] + d[2]]

    gather(0, ring1)
    d0 = gathered(0, ring1)
    tables(0, ring_terms(d0))
    dv[4] = d0[0] + d0[1] + d0[2] + d0[3]
    gather(1, ring2)

    def enc(val, n, h, p, q):
        inv = csi[n, pl.ds(q, 1), :] * rbi[n, h, pl.ds(p, 1), :]
        return jnp.round(val * inv).astype(jnp.int32).astype(jnp.int16)

    def dec(val, n, h, p, q):
        sc = cs[n, pl.ds(q, 1), :] * rb[n, h, pl.ds(p, 1), :]
        return val.astype(jnp.int32).astype(f32) * sc

    def where(t, u, m):
        r = row_of(t, u)
        p = r // 2
        k = (p + c) % 2 + 2 * m
        return r % 2, p, (p + k) % 8, k + p // 4 <= 4

    def ktile(h, p, q):
        rows = ft[p, pl.ds(pl.multiple_of(h * TR, 64), TR), :]
        return jnp.dot(rows, fb[q], preferred_element_type=f32)

    tp, tm, tf = (me1 + 1) % 4, (me1 + 3) % 4, (me1 + 2) % 4

    def slot(j):
        ju = j // 3
        off = (2 + 3 * ju + 3 * (ju // 2) - 2 * (ju // 3)) % 4
        return (me2 + off) % 4, j % 3

    def far1(i, half_at):
        rows = pl.ds(half_at * HR, HR)
        dst = 0 if half_at == 0 else 1
        return rcopy(s1f.at[i, rows], r1f.at[dst, i], q1fs.at[i, half_at], q1fr.at[dst, i],
                     ring1(1 if half_at == 0 else 3))

    def near1(i, way):
        return rcopy(s1n.at[way, i], r1n.at[way, i], q1ns.at[way, i], q1nr.at[way, i],
                     ring1(1 if way == 0 else 3))

    @pl.loop(0, 12)
    def _(j):
        u, m = slot(j)
        h, p, q, ok = where(tf, u, m)
        i = u * 3 + m

        @pl.when(ok)
        def _():
            s1f[i] = enc(ktile(h, p, q), 0, h, p, q)
            far1(i, 0).start()
            far1(i, 1).start()

    @pl.loop(0, 12)
    def _(j):
        u, m = slot(j)
        i = u * 3 + m
        for way, t in ((0, tp), (1, tm)):
            h, p, q, ok = where(t, u, m)

            @pl.when(ok)
            def _():
                tile = ktile(h, p, q)
                far1(i, way).wait_recv()
                add = dec(r1f[way, i], 1 + way, h, p, q)
                low, high = tile[:HR], tile[HR:]
                if way == 0:
                    low = low + add
                else:
                    high = high + add
                s1n[way, i, 0:HR, :] = enc(low, 3 + way, h, p, q)
                s1n[way, i, HR:TR, :] = enc(high, 3 + way, h, p, q)
                near1(i, way).start()

    d1 = gathered(1, ring2)
    tables(7, ring_terms(d1))
    dv[8] = d1[0] + d1[1] + d1[2] + d1[3]

    def zline(o):
        return zdev(o, c)

    gather(2, zline)

    def own1(u, m, then):
        h, p, q, ok = where(me1, u, m)
        i = u * 3 + m

        @pl.when(ok)
        def _():
            tile = ktile(h, p, q)
            near1(i, 0).wait_recv()
            near1(i, 1).wait_recv()
            tile = tile + dec(r1n[0, i], 5, h, p, q) + dec(r1n[1, i], 6, h, p, q)
            then(tile, h, p, q)

    def far2(m, half_at):
        rows = pl.ds(half_at * HR, HR)
        dst = 0 if half_at == 0 else 1
        return rcopy(s2f.at[m, rows], r2f.at[dst, m], q2fs.at[m, half_at], q2fr.at[dst, m],
                     ring2(1 if half_at == 0 else 3))

    def near2(m, way):
        return rcopy(s2n.at[way, m], r2n.at[way, m], q2ns.at[way, m], q2nr.at[way, m],
                     ring2(1 if way == 0 else 3))

    uf, up, um = (me2 + 2) % 4, (me2 + 1) % 4, (me2 + 3) % 4

    @pl.loop(0, 3)
    def _(m):
        def then(tile, h, p, q):
            s2f[m] = enc(tile, 7, h, p, q)
            far2(m, 0).start()
            far2(m, 1).start()

        own1(uf, m, then)

    for way, u in ((0, up), (1, um)):
        @pl.loop(0, 3)
        def _(m):
            def then(tile, h, p, q):
                far2(m, way).wait_recv()
                add = dec(r2f[way, m], 8 + way, h, p, q)
                low, high = tile[:HR], tile[HR:]
                if way == 0:
                    low = low + add
                else:
                    high = high + add
                s2n[way, m, 0:HR, :] = enc(low, 10 + way, h, p, q)
                s2n[way, m, HR:TR, :] = enc(high, 10 + way, h, p, q)
                near2(m, way).start()

            own1(u, m, then)

    d2 = gathered(2, zline)
    tables(14, d2)

    def last(m, o):
        return rcopy(s3.at[m], r3.at[o - 1], q3s.at[m], q3r.at[o - 1], zdev(4 - o, c))

    @pl.loop(0, 3)
    def _(m):
        def then(tile, h, p, q):
            near2(m, 0).wait_recv()
            near2(m, 1).wait_recv()
            tile = tile + dec(r2n[0, m], 12, h, p, q) + dec(r2n[1, m], 13, h, p, q)
            kown[m] = tile
            o = (z + 4 - q // 2) % 4

            @pl.when(o > 0)
            def _():
                s3[m] = enc(tile, 14, h, p, q)
                last(m, o).start()

        own1(me2, m, then)

    def mir(h):
        return rcopy(s4.at[h], r4.at[orb % 2], q4s.at[h], q4r.at[orb % 2], (mirror[h][1], mirror[h][0]))

    kk = (aux + 8 - pr) % 8
    owner = kk + pr // 4 <= 4

    @pl.when(owner)
    def _():
        h = orb % 2
        m = kk // 2
        tile = kown[m]
        for o in range(1, 4):
            rcopy(s3.at[0], r3.at[o - 1], q3s.at[0], q3r.at[o - 1], zdev(o, c)).wait_recv()
            tile = tile + dec(r3[o - 1], 14 + o, h, pr, aux)
        out[...] = tile

        @pl.when(has_mirror)
        def _():
            turned = tile.T
            for h2 in range(2):
                s4[h2] = turned[h2 * TR:(h2 + 1) * TR]
                mir(h2).start()

    @pl.when(jnp.logical_not(owner))
    def _():
        for h2 in range(2):
            rcopy(s4.at[0], r4.at[h2], q4s.at[0], q4r.at[h2], (mirror[h2][1], mirror[h2][0])).wait_recv()
        out[...] = jnp.concatenate([r4[0], r4[1]], axis=1)

    for o in range(1, 8):
        krcopy(o).wait_send()

    @pl.loop(0, NCH)
    def _(q):
        relay(q).wait_send()
        for core in range(2):
            near(q, 1, core).wait_send()
            near(q, 3, core).wait_send()
            forward(q, core).wait_send()
        sibling(q).wait_send()
        fcopy(q).wait_send()

    for level, dev in ((0, ring1), (1, ring2), (2, zline)):
        for o in range(1, 4):
            rcopy(dv.at[4 * level], dv.at[4 * level], ds_.at[4 * level + o], dr.at[4 * level], dev(o)).wait_send()

    @pl.loop(0, 12)
    def _(j):
        u, m = j // 3, j % 3

        @pl.when(where(tf, u, m)[3])
        def _():
            far1(j, 0).wait_send()
            far1(j, 1).wait_send()

        for way, t in ((0, tp), (1, tm)):
            @pl.when(where(t, u, m)[3])
            def _():
                near1(j, way).wait_send()

    @pl.loop(0, 3)
    def _(m):
        @pl.when(where(me1, uf, m)[3])
        def _():
            far2(m, 0).wait_send()
            far2(m, 1).wait_send()

        for way, u in ((0, up), (1, um)):
            @pl.when(where(me1, u, m)[3])
            def _():
                near2(m, way).wait_send()

        _, _, q, ok = where(me1, me2, m)
        o = (z + 4 - q // 2) % 4

        @pl.when(jnp.logical_and(ok, o > 0))
        def _():
            last(m, o).wait_send()

    @pl.when(jnp.logical_and(owner, has_mirror))
    def _():
        for h2 in range(2):
            mir(h2).wait_send()


def shards(half, metric, survive):
    bf, f32, i16 = jnp.bfloat16, jnp.float32, jnp.int16
    rows = half.reshape(CH, half.shape[-1])
    mask = jnp.repeat(survive.reshape(-1).astype(bf), 128).reshape(1, -1)
    eye = jnp.eye(3, dtype=bf)
    kron = (metric[:, None, :, None] * eye[None, :, None, :]).reshape(48, CH)
    perm = jnp.asarray(perm_matrix(), bf)
    vm, dma = pltpu.VMEM, pltpu.SemaphoreType.DMA
    scratch = [
        vm((NCH, CH, CH), bf), vm((NCH, CH, CH), bf), vm((NCH, 96, CH), bf), vm((CH, CH), bf),
        vm((NCH, 2 * CH, CH), bf), vm((NCH, CH, 2 * CH), bf),
        vm((12, 8, CH), f32), vm((18, 8, CH), f32), vm((18, 8, CH), f32),
        vm((18, 2, 8, CH), f32), vm((18, 2, 8, CH), f32),
        vm((12, TR, CH), i16), vm((2, 12, TR, CH), i16), vm((2, 12, HR, CH), i16), vm((2, 12, TR, CH), i16),
        vm((3, TR, CH), f32),
        vm((3, TR, CH), i16), vm((2, 3, TR, CH), i16), vm((2, 3, HR, CH), i16), vm((2, 3, TR, CH), i16),
        vm((3, TR, CH), i16), vm((3, TR, CH), i16),
        vm((2, TR, TR), f32), vm((2, TR, TR), f32),
        dma((NCH, 6)), dma((NCH, 8)), dma((NCH,)), dma((NCH,)), dma((NCH, 2)),
        dma((8,)), dma((8,)), dma((NCH,)), dma((NCH,)), dma((12,)), dma((12,)),
        dma((12, 2)), dma((2, 12)), dma((2, 12)), dma((2, 12)),
        dma((3, 2)), dma((2, 3)), dma((2, 3)), dma((2, 3)),
        dma((3,)), dma((3,)), dma((2,)), dma((2,)),
    ]
    return pl.pallas_call(
        kernel,
        out_shape=jax.ShapeDtypeStruct((TR, CH), f32),
        in_specs=[pl.BlockSpec(memory_space=pltpu.VMEM)] * 4,
        out_specs=pl.BlockSpec(memory_space=pltpu.VMEM),
        scratch_shapes=scratch,
        compiler_params=pltpu.CompilerParams(collective_id=0, has_side_effects=True,
                                             vmem_limit_bytes=62 * 1024 * 1024),
    )(rows, mask, kron, perm)


def solution(mesh):
    placed = (P("aux", "orb", None), P("aux", None), P("aux", "orb", None))
    return jax.shard_map(shards, mesh=mesh, in_specs=placed, out_specs=P("orb", "aux"), check_vma=False)
```

time: 420 us -> 113 us (0.27)
  waiting for transfers between devices: 360 us -> 0 us
  Pallas kernels: 0 us -> 106 us
  matrix products: 21.2 us -> 0 us
  local copies, waits for them, and re-layouts: 20.2 us -> 5.07 us
  between operations: 13.2 us -> 0.02 us
    all_gather x2 -> x0, waiting for transfers between devices: 313 us -> none  [the longest x1 218 us: shards(): lax.all_gather(fitted, 'orb', axis=1, tiled=True).reshape(-1, ao_count)]
    pallas_call x0 -> x1, Pallas kernels: none -> 106 us  [shards(): pl.pallas_call(kernel, out_shape=jax.ShapeDtypeStruct((TR, CH), f32), in_...]
    reduce_scatter x2 -> x0, waiting for transfers between devices: 46.4 us -> none  [sum_by_axis(): x = lax.psum_scatter(x, axis, scatter_dimension=dim, tiled=True)]
    dot_general x2 -> x0, matrix products: 21.2 us -> none  [the longest x1 18.5 us: shards(): lax.dot_general(left_rows, flat_rows, (((0,), (0,)), ((), ())), preferred...]
    unnamed x6 -> x5, local copies, waits for them, and re-layouts: 20.1 us -> 2.38 us
  transfers between devices with their start and end apart: 4 -> 0, of which waited for: 4 -> 0; matrix products, arithmetic and copies ran while one was open for 0% -> 0% of each run, Pallas kernels for 0% -> 0%
where the time goes in v1:
time: 113 us; the launch traced here: 112 us
  Pallas kernels  106 us (94%)
  local copies, waits for them, and re-layouts  5.07 us (4%)
    pallas_call x1, Pallas kernels, shards(): pl.pallas_call(kernel, out_shape=jax.ShapeDtypeStruct((TR, CH), f32), in_...  106 us
    mul x1, local copies, waits for them, and re-layouts, shards(): kron = (metric[:, None, :, None] * eye[None, :, None, :]).reshape(48, CH)  2.68 us
    unnamed x5, local copies, waits for them, and re-layouts  2.38 us

profile of v1, /device:TPU:47, one launch (start us, length us, event | category | flops | bytes accessed | tf_op | source)
XLA Modules:
  0.0 112.4 jit_solution(8818382225824885833)
XLA Ops:
  0.0 0.0 copy-start
  0.0 1.0 broadcast_multiply_fusion
  1.1 2.7 %mul.20.kron = bf16[48,384]{1,0:T(8,128)(2,1)} reshape(bf16[16,3,128,3]{3,2,1,0:T(8,128)(2,1)S(1)} %broadcast_multiply_fusion) | data formatting | bytes 73728 | tf_op jit(solution)/shard_map/mul | solution.py:430
  3.7 0.0 copy-done
  3.7 0.1 broadcast_bitcast_fusion
  3.8 0.6 copy.7
  4.4 106.3 %shard_map.46 = f32[192,384]{1,0:T(8,128)} custom-call(bf16[384,3072]{1,0:T(8,128)(2,1)} %bitcast.11, bf16[1,3072]{1,0:T(2,128)(2,1)} %bitcast.12, bf16[48,384]{1,0:T(8,128)(2,1)} %mul.20.kron, bf16[384,384]{1,0:T(8,128)(2,1)} %constant.2.clone.perm), custom_call_target="tpu_custom_call" | custom-call | tf_op jit(solution)/shard_map/pallas_call | solution.py:449
  110.7 1.7 %copy.9 = f32[192,384]{1,0:T(8,128)} copy(f32[192,384]{1,0:T(8,128)} %shard_map.46) | data formatting | bytes 589824
  (2 shorter events, 0.0 us)
Async XLA Ops:
  0.0 3.7 %copy-start = (s32[1,1,24]{2,1,0:T(1,128)S(1)}, s32[1,1,24]{2,1,0:T(1,128)}, u32[]{:S(2)}) copy-start(s32[1,1,24]{2,1,0:T(1,128)} %param.6) | copy-start | bytes 292

commit v2 on v1

--- a/solution.py
+++ b/solution.py
@@ -11,6 +11,7 @@
 NCH = 8
 TR = 192
 HR = 96
+MR = 112
 TOP = 32700.0
 TINY = 1e-36
 
@@ -24,10 +25,28 @@
     return m
 
 
-def kernel(half, mask, kron, perm, out, snd, rcv, rel, m3, fb, ft, dv, cs, csi, rb, rbi,
+def spread(metric):
+    f32, bf = jnp.float32, jnp.bfloat16
+
+    def third(n):
+        return jnp.floor((n.astype(f32) + 0.5) * (1.0 / 3.0))
+
+    def iota(shape, dim):
+        return lax.broadcasted_iota(jnp.int32, shape, dim)
+
+    left = (third(iota((48, 16), 0)) == iota((48, 16), 1).astype(f32)).astype(f32).astype(bf)
+    right = (third(iota((128, CH), 1)) == iota((128, CH), 0).astype(f32)).astype(f32).astype(bf)
+    rows = jnp.dot(left, metric, preferred_element_type=f32).astype(bf)
+    wide = jnp.dot(rows, right, preferred_element_type=f32)
+    a, b = iota((48, CH), 0), iota((48, CH), 1)
+    same = (a.astype(f32) - 3.0 * third(a)) == (b.astype(f32) - 3.0 * third(b))
+    return jnp.where(same, wide, 0.0).astype(bf)
+
+
+def kernel(half, survive, metric, perm, out, block, kron, snd, rcv, rel, m3, fb, ft, dv, cs, csi, rb, rbi,
            s1f, s1n, r1f, r1n, kown, s2f, s2n, r2f, r2n, s3, r3, s4, r4,
            p1s, p1r, rls, rlr, fws, ks, kr, fs, fr, ds_, dr,
-           q1fs, q1fr, q1ns, q1nr, q2fs, q2fr, q2ns, q2nr, q3s, q3r, q4s, q4r):
+           q1fs, q1fr, q1ns, q1nr, q2fs, q2fr, q2ns, q2nr, q3s, q3r, q4s, q4r, lds):
     f32 = jnp.float32
     aux = lax.axis_index("aux")
     orb = lax.axis_index("orb")
@@ -53,6 +72,15 @@
     mirror = [(2 * aux + h, pr) for h in range(2)]
     has_mirror = aux != pr
 
+    def cut(q):
+        return pl.ds(pl.multiple_of(q * CH, 128), CH)
+
+    def load(q):
+        return pltpu.make_async_copy(half.at[:, cut(q)], block.at[q], lds.at[q])
+
+    for q in range(NCH):
+        load(q).start()
+
     bar = pltpu.get_barrier_semaphore()
     for o in range(1, 8):
         pl.semaphore_signal(bar, inc=1, device_id=((aux + o) % 8, orb), device_id_type=MESH)
@@ -60,6 +88,8 @@
         pl.semaphore_signal(bar, inc=1, device_id=ring1(o), device_id_type=MESH)
         pl.semaphore_signal(bar, inc=1, device_id=ring2(o), device_id_type=MESH)
 
+    kron[...] = spread(metric[...])
+
     @pl.when(has_mirror)
     def _():
         for o, a in mirror:
@@ -112,32 +142,50 @@
     def arrival(q, a):
         return rcopy(rcv.at[q, al48(a)], rcv.at[q, al48(a)], p1s.at[q, 0], p1r.at[q, a], (sib, orb))
 
-    def cut(q):
-        return pl.ds(pl.multiple_of(q * CH, 128), CH)
-
-    @pl.loop(0, NCH)
-    def _(q):
-        block = half[:, cut(q)] * mask[:, cut(q)]
-        snd[q] = jnp.dot(perm[...], block, preferred_element_type=f32).astype(jnp.bfloat16)
-        relay(q).start()
+    def gate(q):
+        flags = [jnp.full((1, 128), survive[0, 0, 3 * q + n].astype(f32)) for n in range(3)]
+        return jnp.concatenate(flags, axis=1).astype(jnp.bfloat16)
+
+    def nears(q):
         for core in range(2):
             near(q, 1, core).start()
             near(q, 3, core).start()
+
+    @pl.loop(0, NCH)
+    def _(q):
+        load(q).wait()
+        kept = block[q] * gate(q)
+        snd[q] = jnp.dot(perm[...], kept, preferred_element_type=f32).astype(jnp.bfloat16)
+        relay(q).start()
         sibling(q).start()
         rcv[q, al48(aux), :] = snd[q, al48(aux), :]
+
+    nears(0)
+    nears(1)
+
+    def fcopy(q):
+        return rcopy(fb.at[q, pl.ds(0, CH)], fb.at[q, pl.ds(CH, CH)], fs.at[q], fr.at[q], (sib, orb))
 
     for o in range(1, 8):
         src = (aux + 8 - o) % 8
         rcopy(kron, m3.at[al48(src)], ks.at[o], kr.at[o], (sib, orb)).wait_recv()
-
-    def fcopy(q):
-        return rcopy(fb.at[q, pl.ds(0, CH)], fb.at[q, pl.ds(CH, CH)], fs.at[q], fr.at[q], (sib, orb))
 
     @pl.loop(0, NCH)
     def _(q):
         relay(q).wait_recv()
         for core in range(2):
             forward(q, core).start()
+
+        @pl.when(q < NCH - 2)
+        def _():
+            nears(q + 2)
+
+    def pair(q):
+        fcopy(q).wait_recv()
+        both = fb[q]
+        ft[q] = both.T
+        wide = both.astype(f32)
+        dv[0, pl.ds(q, 1), :] = jnp.sum(wide * wide, axis=0, keepdims=True)
 
     @pl.loop(0, NCH)
     def _(q):
@@ -146,13 +194,11 @@
         fb[q, 0:CH, :] = jnp.dot(m3[...], rcv[q], preferred_element_type=f32).astype(jnp.bfloat16)
         fcopy(q).start()
 
-    @pl.loop(0, NCH)
-    def _(q):
-        fcopy(q).wait_recv()
-        both = fb[q]
-        ft[q] = both.T
-        wide = both.astype(f32)
-        dv[0, pl.ds(q, 1), :] = jnp.sum(wide * wide, axis=0, keepdims=True)
+        @pl.when(q > 0)
+        def _():
+            pair(q - 1)
+
+    pair(NCH - 1)
 
     def tables(first, terms):
         for n, val in enumerate(terms):
@@ -182,6 +228,72 @@
     def ring_terms(d):
         return [d[0], d[3], d[1], d[0] + d[3], d[0] + d[1], d[3] + d[2], d[1] + d[2]]
 
+    def drain(level=9):
+        for o in range(1, 8):
+            krcopy(o).wait_send()
+
+        @pl.loop(0, NCH)
+        def _(q):
+            relay(q).wait_send()
+            for core in range(2):
+                near(q, 1, core).wait_send()
+                near(q, 3, core).wait_send()
+                forward(q, core).wait_send()
+            sibling(q).wait_send()
+            fcopy(q).wait_send()
+
+        if level < 2:
+            return
+
+        for lv, dev in ((0, ring1), (1, ring2), (2, zline))[:level if level > 1 else 0]:
+            for o in range(1, 4):
+                rcopy(dv.at[4 * lv], dv.at[4 * lv], ds_.at[4 * lv + o], dr.at[4 * lv], dev(o)).wait_send()
+        if level < 2:
+            return
+
+        @pl.loop(0, 12)
+        def _(j):
+            u, m = j // 3, j % 3
+
+            @pl.when(where(tf, u, m)[3])
+            def _():
+                far1(j, 0).wait_send()
+                far1(j, 1).wait_send()
+
+            for way, t in ((0, tp), (1, tm)):
+                @pl.when(where(t, u, m)[3])
+                def _():
+                    near1(j, way).wait_send()
+        if level < 3:
+            return
+
+        @pl.loop(0, 3)
+        def _(m):
+            @pl.when(where(me1, uf, m)[3])
+            def _():
+                far2(m, 0).wait_send()
+                far2(m, 1).wait_send()
+
+            for way, u in ((0, up), (1, um)):
+                @pl.when(where(me1, u, m)[3])
+                def _():
+                    near2(m, way).wait_send()
+
+            _, _, q, ok = where(me1, me2, m)
+            o = (z + 4 - q // 2) % 4
+
+            if level >= 4:
+                @pl.when(jnp.logical_and(ok, o > 0))
+                def _():
+                    last(m, o).wait_send()
+        if level < 5:
+            return
+
+        @pl.when(jnp.logical_and(owner, has_mirror))
+        def _():
+            for h2 in range(2):
+                mir(h2).wait_send()
+
     gather(0, ring1)
     d0 = gathered(0, ring1)
     tables(0, ring_terms(d0))
@@ -263,8 +375,6 @@
     def zline(o):
         return zdev(o, c)
 
-    gather(2, zline)
-
     def own1(u, m, then):
         h, p, q, ok = where(me1, u, m)
         i = u * 3 + m
@@ -276,6 +386,8 @@
             near1(i, 1).wait_recv()
             tile = tile + dec(r1n[0, i], 5, h, p, q) + dec(r1n[1, i], 6, h, p, q)
             then(tile, h, p, q)
+
+    gather(2, zline)
 
     def far2(m, half_at):
         rows = pl.ds(half_at * HR, HR)
@@ -357,80 +469,35 @@
         def _():
             turned = tile.T
             for h2 in range(2):
-                s4[h2] = turned[h2 * TR:(h2 + 1) * TR]
+                part = turned[h2 * TR:(h2 + 1) * TR]
+                flat = jnp.concatenate([part[:HR], part[HR:]], axis=1)
+                top = jnp.max(jnp.abs(flat), axis=0, keepdims=True)
+                power = jnp.ceil(jnp.log2(jnp.maximum(top, TINY)))
+                s4[h2, 0:HR, :] = jnp.round(flat * (jnp.exp2(-power) * TOP)).astype(jnp.int32).astype(jnp.int16)
+                s4[h2, HR:MR, :] = jnp.broadcast_to(power, (16, CH)).astype(jnp.int32).astype(jnp.int16)
                 mir(h2).start()
 
     @pl.when(jnp.logical_not(owner))
     def _():
         for h2 in range(2):
             rcopy(s4.at[0], r4.at[h2], q4s.at[0], q4r.at[h2], (mirror[h2][1], mirror[h2][0])).wait_recv()
-        out[...] = jnp.concatenate([r4[0], r4[1]], axis=1)
-
-    for o in range(1, 8):
-        krcopy(o).wait_send()
-
-    @pl.loop(0, NCH)
-    def _(q):
-        relay(q).wait_send()
-        for core in range(2):
-            near(q, 1, core).wait_send()
-            near(q, 3, core).wait_send()
-            forward(q, core).wait_send()
-        sibling(q).wait_send()
-        fcopy(q).wait_send()
-
-    for level, dev in ((0, ring1), (1, ring2), (2, zline)):
-        for o in range(1, 4):
-            rcopy(dv.at[4 * level], dv.at[4 * level], ds_.at[4 * level + o], dr.at[4 * level], dev(o)).wait_send()
-
-    @pl.loop(0, 12)
-    def _(j):
-        u, m = j // 3, j % 3
-
-        @pl.when(where(tf, u, m)[3])
-        def _():
-            far1(j, 0).wait_send()
-            far1(j, 1).wait_send()
-
-        for way, t in ((0, tp), (1, tm)):
-            @pl.when(where(t, u, m)[3])
-            def _():
-                near1(j, way).wait_send()
-
-    @pl.loop(0, 3)
-    def _(m):
-        @pl.when(where(me1, uf, m)[3])
-        def _():
-            far2(m, 0).wait_send()
-            far2(m, 1).wait_send()
-
-        for way, u in ((0, up), (1, um)):
-            @pl.when(where(me1, u, m)[3])
-            def _():
-                near2(m, way).wait_send()
-
-        _, _, q, ok = where(me1, me2, m)
-        o = (z + 4 - q // 2) % 4
-
-        @pl.when(jnp.logical_and(ok, o > 0))
-        def _():
-            last(m, o).wait_send()
-
-    @pl.when(jnp.logical_and(owner, has_mirror))
-    def _():
+        parts = []
         for h2 in range(2):
-            mir(h2).wait_send()
+            power = r4[h2, HR:MR, :].astype(jnp.int32).astype(f32)[0:1]
+            parts.append(r4[h2, 0:HR, :].astype(jnp.int32).astype(f32) * (jnp.exp2(power) * (1.0 / TOP)))
+        out[0:HR, :] = jnp.concatenate([parts[0][:, :TR], parts[1][:, :TR]], axis=1)
+        out[HR:TR, :] = jnp.concatenate([parts[0][:, TR:], parts[1][:, TR:]], axis=1)
+
+    drain()
 
 
 def shards(half, metric, survive):
     bf, f32, i16 = jnp.bfloat16, jnp.float32, jnp.int16
     rows = half.reshape(CH, half.shape[-1])
-    mask = jnp.repeat(survive.reshape(-1).astype(bf), 128).reshape(1, -1)
-    eye = jnp.eye(3, dtype=bf)
-    kron = (metric[:, None, :, None] * eye[None, :, None, :]).reshape(48, CH)
     perm = jnp.asarray(perm_matrix(), bf)
     vm, dma = pltpu.VMEM, pltpu.SemaphoreType.DMA
     scratch = [
+        vm((NCH, CH, CH), bf), vm((48, CH), bf),
         vm((NCH, CH, CH), bf), vm((NCH, CH, CH), bf), vm((NCH, 96, CH), bf), vm((CH, CH), bf),
         vm((NCH, 2 * CH, CH), bf), vm((NCH, CH, 2 * CH), bf),
         vm((12, 8, CH), f32), vm((18, 8, CH), f32), vm((18, 8, CH), f32),
@@ -439,22 +506,23 @@
         vm((3, TR, CH), f32),
         vm((3, TR, CH), i16), vm((2, 3, TR, CH), i16), vm((2, 3, HR, CH), i16), vm((2, 3, TR, CH), i16),
         vm((3, TR, CH), i16), vm((3, TR, CH), i16),
-        vm((2, TR, TR), f32), vm((2, TR, TR), f32),
+        vm((2, MR, CH), i16), vm((2, MR, CH), i16),
         dma((NCH, 6)), dma((NCH, 8)), dma((NCH,)), dma((NCH,)), dma((NCH, 2)),
         dma((8,)), dma((8,)), dma((NCH,)), dma((NCH,)), dma((12,)), dma((12,)),
         dma((12, 2)), dma((2, 12)), dma((2, 12)), dma((2, 12)),
         dma((3, 2)), dma((2, 3)), dma((2, 3)), dma((2, 3)),
-        dma((3,)), dma((3,)), dma((2,)), dma((2,)),
+        dma((3,)), dma((3,)), dma((2,)), dma((2,)), dma((NCH,)),
     ]
     return pl.pallas_call(
         kernel,
         out_shape=jax.ShapeDtypeStruct((TR, CH), f32),
-        in_specs=[pl.BlockSpec(memory_space=pltpu.VMEM)] * 4,
+        in_specs=[pl.BlockSpec(memory_space=pl.ANY), pl.BlockSpec(memory_space=pltpu.SMEM),
+                  pl.BlockSpec(memory_space=pltpu.VMEM), pl.BlockSpec(memory_space=pltpu.VMEM)],
         out_specs=pl.BlockSpec(memory_space=pltpu.VMEM),
         scratch_shapes=scratch,
         compiler_params=pltpu.CompilerParams(collective_id=0, has_side_effects=True,
                                              vmem_limit_bytes=62 * 1024 * 1024),
-    )(rows, mask, kron, perm)
+    )(rows, survive, metric, perm)
 
 
 def solution(mesh):

time: 113 us -> 99.2 us (0.88)
  Pallas kernels: 106 us -> 97.1 us
  local copies, waits for them, and re-layouts: 5.07 us -> 1.69 us
    pallas_call x1, Pallas kernels: 106 us -> 97.1 us  [shards(): pl.pallas_call(kernel, out_shape=jax.ShapeDtypeStruct((TR, CH), f32), in_...]
    mul x1 -> x0, local copies, waits for them, and re-layouts: 2.68 us -> none  [shards(): kron = (metric[:, None, :, None] * eye[None, :, None, :]).reshape(48, CH)]
    unnamed x5 -> x1, local copies, waits for them, and re-layouts: 2.38 us -> 1.69 us
where the time goes in v2:
time: 99.2 us; the launch traced here: 98.8 us
  Pallas kernels  97.1 us (98%)
  local copies, waits for them, and re-layouts  1.69 us (2%)
    pallas_call x1, Pallas kernels, shards(): pl.pallas_call(kernel, out_shape=jax.ShapeDtypeStruct((TR, CH), f32), in_...  97.1 us

profile of v2, /device:TPU:47, one launch (start us, length us, event | category | flops | bytes accessed | tf_op | source)
XLA Modules:
  0.0 98.8 jit_solution(16554653412874994334)
XLA Ops:
  0.0 97.1 %shard_map.46 = f32[192,384]{1,0:T(8,128)} custom-call(bf16[384,3072]{1,0:T(8,128)(2,1)} %bitcast.1, s32[1,1,24]{2,1,0:T(1,128)} %survive.1, bf16[16,128]{1,0:T(8,128)(2,1)} %metric.1, bf16[384,384]{1,0:T(8,128)(2,1)} %constant.2.clone.perm), custom_call_target="tpu_custom_call" | custom-call | tf_op jit(solution)/shard_map/pallas_call | solution.py:516
  97.1 1.7 %copy.6 = f32[192,384]{1,0:T(8,128)} copy(f32[192,384]{1,0:T(8,128)} %shard_map.46) | data formatting | bytes 589824

commit v3 on v1

v3 whole, which is shorter than its diff:
```python
import jax
import jax.numpy as jnp
import numpy as np
from jax import lax
from jax.experimental import pallas as pl
from jax.experimental.pallas import tpu as pltpu
from jax.sharding import PartitionSpec as P

MESH = pl.DeviceIdType.MESH
CH = 384
NCH = 8
TR = 192
HR = 96
MR = 112
TOP = 32700.0
TINY = 1e-36
ORDER = ((2, 0), (2, 1), (1, 0), (3, 0), (1, 1), (3, 1), (0, 1))


def perm_matrix():
    m = np.zeros((CH, CH), np.float32)
    for d in range(8):
        for aux in range(16):
            for i in range(3):
                m[d * 48 + aux * 3 + i, aux * 24 + 3 * d + i] = 1.0
    return m


def spread(metric):
    f32, bf = jnp.float32, jnp.bfloat16

    def third(n):
        return jnp.floor((n.astype(f32) + 0.5) * (1.0 / 3.0))

    def iota(shape, dim):
        return lax.broadcasted_iota(jnp.int32, shape, dim)

    left = (third(iota((48, 16), 0)) == iota((48, 16), 1).astype(f32)).astype(f32).astype(bf)
    right = (third(iota((128, CH), 1)) == iota((128, CH), 0).astype(f32)).astype(f32).astype(bf)
    rows = jnp.dot(left, metric, preferred_element_type=f32).astype(bf)
    wide = jnp.dot(rows, right, preferred_element_type=f32)
    a, b = iota((48, CH), 0), iota((48, CH), 1)
    same = (a.astype(f32) - 3.0 * third(a)) == (b.astype(f32) - 3.0 * third(b))
    return jnp.where(same, wide, 0.0).astype(bf)


def kernel(half, survive, metric, perm, out, block, kron, snd, rcv, m3, fb, ft, dvr, dv, cs, csi, rb, rbi,
           kbuf, s1f, s1n, r1f, r1n, s2f, s2n, r2f, r2n, s3, r3, s4, r4,
           lds, p1s, p1r, ks, kr, fs, fr, d1s, d1r, ds_, dr,
           q1fs, q1fr, q1ns, q1nr, q2fs, q2fr, q2ns, q2nr, q3s, q3r, q4s, q4r):
    f32 = jnp.float32
    aux = lax.axis_index("aux")
    orb = lax.axis_index("orb")
    z, c = aux // 2, aux % 2
    x, y = orb // 4, orb % 4
    me1 = x * (1 - c) + y * c
    me2 = y * (1 - c) + x * c
    sib = 2 * z + 1 - c

    def row_of(t, u):
        return t * (4 - 3 * c) + u * (1 + 3 * c)

    def ring1(o):
        return (aux, row_of((me1 + o) % 4, me2))

    def ring2(o):
        return (aux, row_of(me1, (me2 + o) % 4))

    def zdev(o, core):
        return (2 * ((z + o) % 4) + core, orb)

    pr = orb // 2
    mirror = [(2 * aux + h, pr) for h in range(2)]
    has_mirror = aux != pr

    def cut(q):
        return pl.ds(pl.multiple_of(q * CH, 128), CH)

    def load(q):
        return pltpu.make_async_copy(half.at[:, cut(q)], block.at[q], lds.at[q])

    for q in range(NCH):
        load(q).start()

    bar = pltpu.get_barrier_semaphore()
    for o in range(1, 8):
        pl.semaphore_signal(bar, inc=1, device_id=((aux + o) % 8, orb), device_id_type=MESH)
    for o in range(1, 4):
        pl.semaphore_signal(bar, inc=1, device_id=ring1(o), device_id_type=MESH)
        pl.semaphore_signal(bar, inc=1, device_id=ring2(o), device_id_type=MESH)

    kron[...] = spread(metric[...])

    @pl.when(has_mirror)
    def _():
        for o, a in mirror:
            pl.semaphore_signal(bar, inc=1, device_id=(a, o), device_id_type=MESH)

    def rcopy(src, dst, ss, rs, dev):
        return pltpu.make_async_remote_copy(src_ref=src, dst_ref=dst, send_sem=ss, recv_sem=rs,
                                            device_id=dev, device_id_type=MESH)

    def al48(v):
        return pl.ds(pl.multiple_of(v * 48, 16), 48)

    def krcopy(o):
        dst = m3.at[al48(aux)]
        return rcopy(kron, dst, ks.at[o], kr.at[o], ((aux + o) % 8, orb))

    def send(q, o, flip):
        dev = 2 * ((z + o) % 4) + (c + flip) % 2
        return rcopy(snd.at[q, al48(dev)], rcv.at[q, al48(aux)], p1s.at[q, 2 * o + flip], p1r.at[q, aux], (dev, orb))

    def arrival(q, a):
        return rcopy(rcv.at[q, al48(a)], rcv.at[q, al48(a)], p1s.at[q, 0], p1r.at[q, a], (sib, orb))

    def gate(q):
        flags = [jnp.full((1, 128), survive[0, 0, 3 * q + n].astype(f32)) for n in range(3)]
        return jnp.concatenate(flags, axis=1).astype(jnp.bfloat16)

    @pl.loop(0, NCH)
    def _(q):
        load(q).wait()
        kept = block[q] * gate(q)
        snd[q] = jnp.dot(perm[...], kept, preferred_element_type=f32).astype(jnp.bfloat16)
        rcv[q, al48(aux), :] = snd[q, al48(aux), :]

    @pl.when(has_mirror)
    def _():
        pl.semaphore_wait(bar, 15)

    @pl.when(jnp.logical_not(has_mirror))
    def _():
        pl.semaphore_wait(bar, 13)

    for o in range(1, 8):
        krcopy(o).start()
    m3[al48(aux), :] = kron[...]

    @pl.loop(0, NCH)
    def _(q):
        for o, flip in ORDER:
            send(q, o, flip).start()

    for o in range(1, 8):
        src = (aux + 8 - o) % 8
        rcopy(kron, m3.at[al48(src)], ks.at[o], kr.at[o], (sib, orb)).wait_recv()

    def fcopy(q):
        return rcopy(fb.at[q, pl.ds(0, CH)], fb.at[q, pl.ds(CH, CH)], fs.at[q], fr.at[q], (sib, orb))

    def table(n, val, at):
        val = jnp.maximum(val, TINY)
        lane = lax.broadcasted_iota(jnp.int32, val.shape, 1)
        inv = lax.rsqrt(val)
        csi[n, at, :] = inv
        cs[n, at, :] = val * inv
        for h in range(2):
            part = jnp.where((lane >= TR) == (h == 1), val, TINY)
            top = jnp.broadcast_to(jnp.max(part, axis=1, keepdims=True), val.shape)
            tinv = lax.rsqrt(top)
            rbi[n, h, at, :] = tinv * TOP
            rb[n, h, at, :] = top * tinv * (1.0 / TOP)

    def tables(first, terms):
        for n, val in enumerate(terms):
            table(first + n, val, slice(None))

    def gather(level, dev):
        base = 4 * level
        for o in range(1, 4):
            rcopy(dv.at[base], dv.at[base + 4 - o], ds_.at[base + o], dr.at[base + 4 - o], dev(o)).start()

    def gathered(level, dev):
        base = 4 * level
        for o in range(1, 4):
            rcopy(dv.at[base], dv.at[base + o], ds_.at[base + o], dr.at[base + o], dev(o)).wait_recv()
        return [dv[base + o] for o in range(4)]

    def ring_terms(d):
        return [d[0], d[3], d[1], d[0] + d[3], d[0] + d[1], d[3] + d[2], d[1] + d[2]]

    def dcopy(q, o):
        return rcopy(dvr.at[0, q], dvr.at[4 - o, q], d1s.at[o, q], d1r.at[4 - o, q], ring1(o))

    def enc(val, n, h, p, q):
        inv = csi[n, pl.ds(q, 1), :] * rbi[n, h, pl.ds(p, 1), :]
        return jnp.round(val * inv).astype(jnp.int32).astype(jnp.int16)

    def dec(val, n, h, p, q):
        sc = cs[n, pl.ds(q, 1), :] * rb[n, h, pl.ds(p, 1), :]
        return val.astype(jnp.int32).astype(f32) * sc

    def where(t, u, m):
        r = row_of(t, u)
        p = r // 2
        k = (p + c) % 2 + 2 * m
        return r % 2, p, (p + k) % 8, k + p // 4 <= 4

    tp, tm, tf = (me1 + 1) % 4, (me1 + 3) % 4, (me1 + 2) % 4

    def pair_of(k, j):
        g = (k - j) // 5
        return j + g * (k - j), k - g * (k - j)

    def place(p, q, h):
        a, b = p // 2, 2 * (p % 2) + h
        t, u = a * (1 - c) + b * c, b * (1 - c) + a * c
        return u * 3 + ((q - p + 8) % 8) // 2, (t - me1 + 4) % 4

    def each(k, body):
        @pl.loop(0, k + 1)
        def _(j):
            p, q = pair_of(k, j)

            @pl.when(q % 2 == c)
            def _():
                body(p, q)

    def far1(i, half_at):
        rows = pl.ds(half_at * HR, HR)
        dst = 0 if half_at == 0 else 1
        return rcopy(s1f.at[i, rows], r1f.at[dst, i], q1fs.at[i, half_at], q1fr.at[dst, i],
                     ring1(1 if half_at == 0 else 3))

    def near1(i, way, dev):
        return rcopy(s1n.at[way, i], r1n.at[way, i], q1ns.at[way, i], q1nr.at[way, i], dev)

    def pair(k):
        fcopy(k).wait_recv()
        both = fb[k]
        ft[k] = both.T
        wide = both.astype(f32)
        norm = jnp.sum(wide * wide, axis=0, keepdims=True)
        dvr[0, k] = norm
        for o in range(1, 4):
            dcopy(k, o).start()
        table(0, norm, pl.ds(k, 1))

    def compute(k):
        def body(p, q):
            tile = jnp.dot(ft[p], fb[q], preferred_element_type=f32)
            for h in range(2):
                i, role = place(p, q, h)
                part = tile[h * TR:(h + 1) * TR]

                @pl.when(role == 2)
                def _():
                    s1f[i] = enc(part, 0, h, p, q)
                    far1(i, 0).start()
                    far1(i, 1).start()

                @pl.when(role != 2)
                def _():
                    kbuf[(role + 1) // 2, i] = part

        each(k, body)

    def norms(k):
        for o in range(1, 4):
            rcopy(dvr.at[0, k], dvr.at[o, k], d1s.at[o, k], d1r.at[o, k], ring1(o)).wait_recv()
        d = [dvr[o, k] for o in range(4)]
        for n, val in enumerate(ring_terms(d)):
            if n:
                table(n, val, pl.ds(k, 1))
        dv[4, pl.ds(k, 1), :] = d[0] + d[1] + d[2] + d[3]

    def pass_on(k):
        def body(p, q):
            for h in range(2):
                i, role = place(p, q, h)

                @pl.when(role % 2 == 1)
                def _():
                    way = role // 2
                    pltpu.make_async_remote_copy(
                        src_ref=s1f.at[i, pl.ds(0, HR)], dst_ref=r1f.at[way, i], send_sem=q1fs.at[i, 0],
                        recv_sem=q1fr.at[way, i], device_id=ring1(1), device_id_type=MESH).wait_recv()
                    rows = pl.ds(pl.multiple_of(way * HR, 32), HR)
                    kbuf[1 + way, i, rows, :] = kbuf[1 + way, i, rows, :] + dec(r1f[way, i], 1 + way, h, p, q)
                    s1n[way, i] = enc(kbuf[1 + way, i], 3 + way, h, p, q)
                    near1(i, way, ring1(role)).start()

        each(k, body)

    def collect(k):
        def body(p, q):
            for h in range(2):
                i, role = place(p, q, h)

                @pl.when(role == 0)
                def _():
                    near1(i, 0, ring1(1)).wait_recv()
                    near1(i, 1, ring1(1)).wait_recv()
                    kbuf[0, i] = kbuf[0, i] + dec(r1n[0, i], 5, h, p, q) + dec(r1n[1, i], 6, h, p, q)

        each(k, body)

    @pl.loop(0, NCH)
    def _(k):
        for o in range(1, 8):
            arrival(k, (aux + o) % 8).wait_recv()
        fb[k, 0:CH, :] = jnp.dot(m3[...], rcv[k], preferred_element_type=f32).astype(jnp.bfloat16)
        fcopy(k).start()

        @pl.when(k > 0)
        def _():
            norms(k - 1)
            pass_on(k - 1)

        @pl.when(k > 1)
        def _():
            collect(k - 2)

        pair(k)
        compute(k)

    norms(NCH - 1)
    gather(1, ring2)
    pass_on(NCH - 1)
    collect(NCH - 2)
    d1 = gathered(1, ring2)
    tables(7, ring_terms(d1))
    dv[8] = d1[0] + d1[1] + d1[2] + d1[3]

    def zline(o):
        return zdev(o, c)

    gather(2, zline)
    collect(NCH - 1)

    def own1(u, m, then):
        h, p, q, ok = where(me1, u, m)

        @pl.when(ok)
        def _():
            then(kbuf[0, u * 3 + m], h, p, q)

    def far2(m, half_at):
        rows = pl.ds(half_at * HR, HR)
        dst = 0 if half_at == 0 else 1
        return rcopy(s2f.at[m, rows], r2f.at[dst, m], q2fs.at[m, half_at], q2fr.at[dst, m],
                     ring2(1 if half_at == 0 else 3))

    def near2(m, way):
        return rcopy(s2n.at[way, m], r2n.at[way, m], q2ns.at[way, m], q2nr.at[way, m],
                     ring2(1 if way == 0 else 3))

    uf, up, um = (me2 + 2) % 4, (me2 + 1) % 4, (me2 + 3) % 4

    @pl.loop(0, 3)
    def _(m):
        def then(tile, h, p, q):
            s2f[m] = enc(tile, 7, h, p, q)
            far2(m, 0).start()
            far2(m, 1).start()

        own1(uf, m, then)

    for way, u in ((0, up), (1, um)):
        @pl.loop(0, 3)
        def _(m):
            def then(tile, h, p, q):
                far2(m, way).wait_recv()
                add = dec(r2f[way, m], 8 + way, h, p, q)
                low, high = tile[:HR], tile[HR:]
                if way == 0:
                    low = low + add
                else:
                    high = high + add
                s2n[way, m, 0:HR, :] = enc(low, 10 + way, h, p, q)
                s2n[way, m, HR:TR, :] = enc(high, 10 + way, h, p, q)
                near2(m, way).start()

            own1(u, m, then)

    d2 = gathered(2, zline)
    tables(14, d2)

    def last(m, o):
        return rcopy(s3.at[m], r3.at[o - 1], q3s.at[m], q3r.at[o - 1], zdev(4 - o, c))

    @pl.loop(0, 3)
    def _(m):
        def then(tile, h, p, q):
            near2(m, 0).wait_recv()
            near2(m, 1).wait_recv()
            tile = tile + dec(r2n[0, m], 12, h, p, q) + dec(r2n[1, m], 13, h, p, q)
            kbuf[0, me2 * 3 + m] = tile
            o = (z + 4 - q // 2) % 4

            @pl.when(o > 0)
            def _():
                s3[m] = enc(tile, 14, h, p, q)
                last(m, o).start()

        own1(me2, m, then)

    def mir(h):
        return rcopy(s4.at[h], r4.at[orb % 2], q4s.at[h], q4r.at[orb % 2], (mirror[h][1], mirror[h][0]))

    kk = (aux + 8 - pr) % 8
    owner = kk + pr // 4 <= 4

    @pl.when(owner)
    def _():
        h = orb % 2
        m = kk // 2
        tile = kbuf[0, me2 * 3 + m]
        for o in range(1, 4):
            rcopy(s3.at[0], r3.at[o - 1], q3s.at[0], q3r.at[o - 1], zdev(o, c)).wait_recv()
            tile = tile + dec(r3[o - 1], 14 + o, h, pr, aux)
        out[...] = tile

        @pl.when(has_mirror)
        def _():
            turned = tile.T
            for h2 in range(2):
                part = turned[h2 * TR:(h2 + 1) * TR]
                flat = jnp.concatenate([part[:HR], part[HR:]], axis=1)
                top = jnp.max(jnp.abs(flat), axis=0, keepdims=True)
                power = jnp.ceil(jnp.log2(jnp.maximum(top, TINY)))
                s4[h2, 0:HR, :] = jnp.round(flat * (jnp.exp2(-power) * TOP)).astype(jnp.int32).astype(jnp.int16)
                s4[h2, HR:MR, :] = jnp.broadcast_to(power, (16, CH)).astype(jnp.int32).astype(jnp.int16)
                mir(h2).start()

    @pl.when(jnp.logical_not(owner))
    def _():
        for h2 in range(2):
            rcopy(s4.at[0], r4.at[h2], q4s.at[0], q4r.at[h2], (mirror[h2][1], mirror[h2][0])).wait_recv()
        parts = []
        for h2 in range(2):
            power = r4[h2, HR:MR, :].astype(jnp.int32).astype(f32)[0:1]
            parts.append(r4[h2, 0:HR, :].astype(jnp.int32).astype(f32) * (jnp.exp2(power) * (1.0 / TOP)))
        out[0:HR, :] = jnp.concatenate([parts[0][:, :TR], parts[1][:, :TR]], axis=1)
        out[HR:TR, :] = jnp.concatenate([parts[0][:, TR:], parts[1][:, TR:]], axis=1)

    for o in range(1, 8):
        krcopy(o).wait_send()

    @pl.loop(0, NCH)
    def _(q):
        for o, flip in ORDER:
            send(q, o, flip).wait_send()
        fcopy(q).wait_send()
        for o in range(1, 4):
            dcopy(q, o).wait_send()

    for level, dev in ((1, ring2), (2, zline)):
        for o in range(1, 4):
            rcopy(dv.at[4 * level], dv.at[4 * level], ds_.at[4 * level + o], dr.at[4 * level], dev(o)).wait_send()

    @pl.loop(0, 12)
    def _(j):
        u, m = j // 3, j % 3

        @pl.when(where(tf, u, m)[3])
        def _():
            far1(j, 0).wait_send()
            far1(j, 1).wait_send()

        for way, t in ((0, tp), (1, tm)):
            @pl.when(where(t, u, m)[3])
            def _():
                near1(j, way, ring1(1)).wait_send()

    @pl.loop(0, 3)
    def _(m):
        @pl.when(where(me1, uf, m)[3])
        def _():
            far2(m, 0).wait_send()
            far2(m, 1).wait_send()

        for way, u in ((0, up), (1, um)):
            @pl.when(where(me1, u, m)[3])
            def _():
                near2(m, way).wait_send()

        _, _, q, ok = where(me1, me2, m)
        o = (z + 4 - q // 2) % 4

        @pl.when(jnp.logical_and(ok, o > 0))
        def _():
            last(m, o).wait_send()

    @pl.when(jnp.logical_and(owner, has_mirror))
    def _():
        for h2 in range(2):
            mir(h2).wait_send()


def shards(half, metric, survive):
    bf, f32, i16 = jnp.bfloat16, jnp.float32, jnp.int16
    rows = half.reshape(CH, half.shape[-1])
    perm = jnp.asarray(perm_matrix(), bf)
    vm, dma = pltpu.VMEM, pltpu.SemaphoreType.DMA
    scratch = [
        vm((NCH, CH, CH), bf), vm((48, CH), bf),
        vm((NCH, CH, CH), bf), vm((NCH, CH, CH), bf), vm((CH, CH), bf),
        vm((NCH, 2 * CH, CH), bf), vm((NCH, CH, 2 * CH), bf),
        vm((4, NCH, 1, CH), f32), vm((12, 8, CH), f32), vm((18, 8, CH), f32), vm((18, 8, CH), f32),
        vm((18, 2, 8, CH), f32), vm((18, 2, 8, CH), f32),
        vm((3, 12, TR, CH), f32),
        vm((12, TR, CH), i16), vm((2, 12, TR, CH), i16), vm((2, 12, HR, CH), i16), vm((2, 12, TR, CH), i16),
        vm((3, TR, CH), i16), vm((2, 3, TR, CH), i16), vm((2, 3, HR, CH), i16), vm((2, 3, TR, CH), i16),
        vm((3, TR, CH), i16), vm((3, TR, CH), i16),
        vm((2, MR, CH), i16), vm((2, MR, CH), i16),
        dma((NCH,)), dma((NCH, 8)), dma((NCH, 8)), dma((8,)), dma((8,)), dma((NCH,)), dma((NCH,)),
        dma((4, NCH)), dma((4, NCH)), dma((12,)), dma((12,)),
        dma((12, 2)), dma((2, 12)), dma((2, 12)), dma((2, 12)),
        dma((3, 2)), dma((2, 3)), dma((2, 3)), dma((2, 3)),
        dma((3,)), dma((3,)), dma((2,)), dma((2,)),
    ]
    return pl.pallas_call(
        kernel,
        out_shape=jax.ShapeDtypeStruct((TR, CH), f32),
        in_specs=[pl.BlockSpec(memory_space=pl.ANY), pl.BlockSpec(memory_space=pltpu.SMEM),
                  pl.BlockSpec(memory_space=pltpu.VMEM), pl.BlockSpec(memory_space=pltpu.VMEM)],
        out_specs=pl.BlockSpec(memory_space=pltpu.VMEM),
        scratch_shapes=scratch,
        compiler_params=pltpu.CompilerParams(collective_id=0, has_side_effects=True,
                                             vmem_limit_bytes=62 * 1024 * 1024),
    )(rows, survive, metric, perm)


def solution(mesh):
    placed = (P("aux", "orb", None), P("aux", None), P("aux", "orb", None))
    return jax.shard_map(shards, mesh=mesh, in_specs=placed, out_specs=P("orb", "aux"), check_vma=False)
```

time: 113 us -> 121 us (1.071)
  the two profiles are of different devices: /device:TPU:47 before, /device:TPU:107 now
where the time goes in v3:
time: 121 us
  Pallas kernels  119 us (98%)
  local copies, waits for them, and re-layouts  1.69 us (1%)
    pallas_call x1, Pallas kernels, shards(): pl.pallas_call(kernel, out_shape=jax.ShapeDtypeStruct((TR, CH), f32), in_...  119 us

profile of v3, /device:TPU:107, one launch (start us, length us, event | category | flops | bytes accessed | tf_op | source)
XLA Modules:
  0.0 121.1 jit_solution(8291515771294762930)
XLA Ops:
  0.0 119.4 %shard_map.46 = f32[192,384]{1,0:T(8,128)} custom-call(bf16[384,3072]{1,0:T(8,128)(2,1)} %bitcast.1, s32[1,1,24]{2,1,0:T(1,128)} %survive.1, bf16[16,128]{1,0:T(8,128)(2,1)} %metric.1, bf16[384,384]{1,0:T(8,128)(2,1)} %constant.2.clone.perm), custom_call_target="tpu_custom_call" | custom-call | tf_op jit(solution)/shard_map/pallas_call | solution.py:514
  119.4 1.7 %copy.6 = f32[192,384]{1,0:T(8,128)} copy(f32[192,384]{1,0:T(8,128)} %shard_map.46) | data formatting | bytes 589824

commit v4 on v3

--- a/solution.py
+++ b/solution.py
@@ -44,7 +44,7 @@
     return jnp.where(same, wide, 0.0).astype(bf)
 
 
-def kernel(half, survive, metric, perm, out, block, kron, snd, rcv, m3, fb, ft, dvr, dv, cs, csi, rb, rbi,
+def kernel(half, survive, metric, perm, out, block, kron, snd, rcv, m3, fb, ft, dvr, dv, cs1, csi1, rb1, rbi1, cs, csi, rb, rbi,
            kbuf, s1f, s1n, r1f, r1n, s2f, s2n, r2f, r2n, s3, r3, s4, r4,
            lds, p1s, p1r, ks, kr, fs, fr, d1s, d1r, ds_, dr,
            q1fs, q1fr, q1ns, q1nr, q2fs, q2fr, q2ns, q2nr, q3s, q3r, q4s, q4r):
@@ -149,22 +149,31 @@
     def fcopy(q):
         return rcopy(fb.at[q, pl.ds(0, CH)], fb.at[q, pl.ds(CH, CH)], fs.at[q], fr.at[q], (sib, orb))
 
-    def table(n, val, at):
+    def scales(val):
         val = jnp.maximum(val, TINY)
         lane = lax.broadcasted_iota(jnp.int32, val.shape, 1)
         inv = lax.rsqrt(val)
-        csi[n, at, :] = inv
-        cs[n, at, :] = val * inv
+        yield val * inv, inv
         for h in range(2):
             part = jnp.where((lane >= TR) == (h == 1), val, TINY)
             top = jnp.broadcast_to(jnp.max(part, axis=1, keepdims=True), val.shape)
             tinv = lax.rsqrt(top)
-            rbi[n, h, at, :] = tinv * TOP
-            rb[n, h, at, :] = top * tinv * (1.0 / TOP)
+            yield top * tinv * (1.0 / TOP), tinv * TOP
+
+    def tables1(k, rows, val):
+        for n, (sc, inv) in enumerate(scales(val)):
+            if n == 0:
+                cs1[k, rows, :], csi1[k, rows, :] = sc, inv
+            else:
+                rb1[n - 1, k, rows, :], rbi1[n - 1, k, rows, :] = sc, inv
 
     def tables(first, terms):
-        for n, val in enumerate(terms):
-            table(first + n, val, slice(None))
+        for i, val in enumerate(terms):
+            for n, (sc, inv) in enumerate(scales(val)):
+                if n == 0:
+                    cs[first + i], csi[first + i] = sc, inv
+                else:
+                    rb[first + i, n - 1], rbi[first + i, n - 1] = sc, inv
 
     def gather(level, dev):
         base = 4 * level
@@ -182,6 +191,14 @@
 
     def dcopy(q, o):
         return rcopy(dvr.at[0, q], dvr.at[4 - o, q], d1s.at[o, q], d1r.at[4 - o, q], ring1(o))
+
+    def enc1(val, n, h, p, q):
+        inv = csi1[q, pl.ds(n, 1), :] * rbi1[h, p, pl.ds(n, 1), :]
+        return jnp.round(val * inv).astype(jnp.int32).astype(jnp.int16)
+
+    def dec1(val, n, h, p, q):
+        sc = cs1[q, pl.ds(n, 1), :] * rb1[h, p, pl.ds(n, 1), :]
+        return val.astype(jnp.int32).astype(f32) * sc
 
     def enc(val, n, h, p, q):
         inv = csi[n, pl.ds(q, 1), :] * rbi[n, h, pl.ds(p, 1), :]
@@ -235,7 +252,7 @@
         dvr[0, k] = norm
         for o in range(1, 4):
             dcopy(k, o).start()
-        table(0, norm, pl.ds(k, 1))
+        tables1(k, pl.ds(0, 1), norm)
 
     def compute(k):
         def body(p, q):
@@ -246,7 +263,7 @@
 
                 @pl.when(role == 2)
                 def _():
-                    s1f[i] = enc(part, 0, h, p, q)
+                    s1f[i] = enc1(part, 0, h, p, q)
                     far1(i, 0).start()
                     far1(i, 1).start()
 
@@ -260,10 +277,9 @@
         for o in range(1, 4):
             rcopy(dvr.at[0, k], dvr.at[o, k], d1s.at[o, k], d1r.at[o, k], ring1(o)).wait_recv()
         d = [dvr[o, k] for o in range(4)]
-        for n, val in enumerate(ring_terms(d)):
-            if n:
-                table(n, val, pl.ds(k, 1))
-        dv[4, pl.ds(k, 1), :] = d[0] + d[1] + d[2] + d[3]
+        whole = d[0] + d[1] + d[2] + d[3]
+        tables1(k, slice(None), jnp.concatenate(ring_terms(d) + [whole], axis=0))
+        dv[4, pl.ds(k, 1), :] = whole
 
     def pass_on(k):
         def body(p, q):
@@ -277,8 +293,8 @@
                         src_ref=s1f.at[i, pl.ds(0, HR)], dst_ref=r1f.at[way, i], send_sem=q1fs.at[i, 0],
                         recv_sem=q1fr.at[way, i], device_id=ring1(1), device_id_type=MESH).wait_recv()
                     rows = pl.ds(pl.multiple_of(way * HR, 32), HR)
-                    kbuf[1 + way, i, rows, :] = kbuf[1 + way, i, rows, :] + dec(r1f[way, i], 1 + way, h, p, q)
-                    s1n[way, i] = enc(kbuf[1 + way, i], 3 + way, h, p, q)
+                    kbuf[1 + way, i, rows, :] = kbuf[1 + way, i, rows, :] + dec1(r1f[way, i], 1 + way, h, p, q)
+                    s1n[way, i] = enc1(kbuf[1 + way, i], 3 + way, h, p, q)
                     near1(i, way, ring1(role)).start()
 
         each(k, body)
@@ -292,7 +308,7 @@
                 def _():
                     near1(i, 0, ring1(1)).wait_recv()
                     near1(i, 1, ring1(1)).wait_recv()
-                    kbuf[0, i] = kbuf[0, i] + dec(r1n[0, i], 5, h, p, q) + dec(r1n[1, i], 6, h, p, q)
+                    kbuf[0, i] = kbuf[0, i] + dec1(r1n[0, i], 5, h, p, q) + dec1(r1n[1, i], 6, h, p, q)
 
         each(k, body)
 
@@ -303,24 +319,27 @@
         fb[k, 0:CH, :] = jnp.dot(m3[...], rcv[k], preferred_element_type=f32).astype(jnp.bfloat16)
         fcopy(k).start()
 
-        @pl.when(k > 0)
-        def _():
-            norms(k - 1)
-            pass_on(k - 1)
-
         @pl.when(k > 1)
         def _():
-            collect(k - 2)
+            norms(k - 2)
+            pass_on(k - 2)
+
+        @pl.when(k > 2)
+        def _():
+            collect(k - 3)
 
         pair(k)
         compute(k)
 
+    norms(NCH - 2)
     norms(NCH - 1)
     gather(1, ring2)
+    pass_on(NCH - 2)
+    collect(NCH - 3)
     pass_on(NCH - 1)
     collect(NCH - 2)
     d1 = gathered(1, ring2)
-    tables(7, ring_terms(d1))
+    tables(0, ring_terms(d1))
     dv[8] = d1[0] + d1[1] + d1[2] + d1[3]
 
     def zline(o):
@@ -351,7 +370,7 @@
     @pl.loop(0, 3)
     def _(m):
         def then(tile, h, p, q):
-            s2f[m] = enc(tile, 7, h, p, q)
+            s2f[m] = enc(tile, 0, h, p, q)
             far2(m, 0).start()
             far2(m, 1).start()
 
@@ -362,20 +381,20 @@
         def _(m):
             def then(tile, h, p, q):
                 far2(m, way).wait_recv()
-                add = dec(r2f[way, m], 8 + way, h, p, q)
+                add = dec(r2f[way, m], 1 + way, h, p, q)
                 low, high = tile[:HR], tile[HR:]
                 if way == 0:
                     low = low + add
                 else:
                     high = high + add
-                s2n[way, m, 0:HR, :] = enc(low, 10 + way, h, p, q)
-                s2n[way, m, HR:TR, :] = enc(high, 10 + way, h, p, q)
+                s2n[way, m, 0:HR, :] = enc(low, 3 + way, h, p, q)
+                s2n[way, m, HR:TR, :] = enc(high, 3 + way, h, p, q)
                 near2(m, way).start()
 
             own1(u, m, then)
 
     d2 = gathered(2, zline)
-    tables(14, d2)
+    tables(7, d2)
 
     def last(m, o):
         return rcopy(s3.at[m], r3.at[o - 1], q3s.at[m], q3r.at[o - 1], zdev(4 - o, c))
@@ -385,13 +404,13 @@
         def then(tile, h, p, q):
             near2(m, 0).wait_recv()
             near2(m, 1).wait_recv()
-            tile = tile + dec(r2n[0, m], 12, h, p, q) + dec(r2n[1, m], 13, h, p, q)
+            tile = tile + dec(r2n[0, m], 5, h, p, q) + dec(r2n[1, m], 6, h, p, q)
             kbuf[0, me2 * 3 + m] = tile
             o = (z + 4 - q // 2) % 4
 
             @pl.when(o > 0)
             def _():
-                s3[m] = enc(tile, 14, h, p, q)
+                s3[m] = enc(tile, 7, h, p, q)
                 last(m, o).start()
 
         own1(me2, m, then)
@@ -409,7 +428,7 @@
         tile = kbuf[0, me2 * 3 + m]
         for o in range(1, 4):
             rcopy(s3.at[0], r3.at[o - 1], q3s.at[0], q3r.at[o - 1], zdev(o, c)).wait_recv()
-            tile = tile + dec(r3[o - 1], 14 + o, h, pr, aux)
+            tile = tile + dec(r3[o - 1], 7 + o, h, pr, aux)
         out[...] = tile
 
         @pl.when(has_mirror)
@@ -498,8 +517,9 @@
         vm((NCH, CH, CH), bf), vm((48, CH), bf),
         vm((NCH, CH, CH), bf), vm((NCH, CH, CH), bf), vm((CH, CH), bf),
         vm((NCH, 2 * CH, CH), bf), vm((NCH, CH, 2 * CH), bf),
-        vm((4, NCH, 1, CH), f32), vm((12, 8, CH), f32), vm((18, 8, CH), f32), vm((18, 8, CH), f32),
-        vm((18, 2, 8, CH), f32), vm((18, 2, 8, CH), f32),
+        vm((4, NCH, 1, CH), f32), vm((12, 8, CH), f32),
+        vm((NCH, 8, CH), f32), vm((NCH, 8, CH), f32), vm((2, NCH, 8, CH), f32), vm((2, NCH, 8, CH), f32),
+        vm((11, 8, CH), f32), vm((11, 8, CH), f32), vm((11, 2, 8, CH), f32), vm((11, 2, 8, CH), f32),
         vm((3, 12, TR, CH), f32),
         vm((12, TR, CH), i16), vm((2, 12, TR, CH), i16), vm((2, 12, HR, CH), i16), vm((2, 12, TR, CH), i16),
         vm((3, TR, CH), i16), vm((2, 3, TR, CH), i16), vm((2, 3, HR, CH), i16), vm((2, 3, TR, CH), i16),

time: 121 us -> 110 us (0.909)
  the two profiles are of different devices: /device:TPU:107 before, /device:TPU:96 now
where the time goes in v4:
time: 110 us; the launch traced here: 109 us
  Pallas kernels  108 us (98%)
  local copies, waits for them, and re-layouts  1.69 us (2%)
    pallas_call x1, Pallas kernels, shards(): pl.pallas_call(kernel, out_shape=jax.ShapeDtypeStruct((TR, CH), f32), in_...  108 us

profile of v4, /device:TPU:96, one launch (start us, length us, event | category | flops | bytes accessed | tf_op | source)
XLA Modules:
  0.0 109.4 jit_solution(2725725673740350730)
XLA Ops:
  0.0 107.7 %shard_map.46 = f32[192,384]{1,0:T(8,128)} custom-call(bf16[384,3072]{1,0:T(8,128)(2,1)} %bitcast.1, s32[1,1,24]{2,1,0:T(1,128)} %survive.1, bf16[16,128]{1,0:T(8,128)(2,1)} %metric.1, bf16[384,384]{1,0:T(8,128)(2,1)} %constant.2.clone.perm), custom_call_target="tpu_custom_call" | custom-call | tf_op jit(solution)/shard_map/pallas_call | solution.py:534
  107.7 1.7 %copy.6 = f32[192,384]{1,0:T(8,128)} copy(f32[192,384]{1,0:T(8,128)} %shard_map.46) | data formatting | bytes 589824

commit v5 on v4

--- a/solution.py
+++ b/solution.py
@@ -1,6 +1,5 @@
 import jax
 import jax.numpy as jnp
-import numpy as np
 from jax import lax
 from jax.experimental import pallas as pl
 from jax.experimental.pallas import tpu as pltpu
@@ -17,35 +16,34 @@
 ORDER = ((2, 0), (2, 1), (1, 0), (3, 0), (1, 1), (3, 1), (0, 1))
 
 
-def perm_matrix():
-    m = np.zeros((CH, CH), np.float32)
-    for d in range(8):
-        for aux in range(16):
-            for i in range(3):
-                m[d * 48 + aux * 3 + i, aux * 24 + 3 * d + i] = 1.0
-    return m
+def third(n):
+    return jnp.floor((n + 0.5) * (1.0 / 3.0))
+
+
+def iota(shape, dim):
+    return lax.broadcasted_iota(jnp.int32, shape, dim).astype(jnp.float32)
+
+
+def sorting():
+    row, col = iota((CH, CH), 0), iota((CH, CH), 1)
+    d = jnp.floor((row + 0.5) * (1.0 / 48.0))
+    rest = row - 48.0 * d
+    aux = third(rest)
+    return jnp.where(col == 21.0 * aux + 3.0 * d + rest, 1.0, 0.0).astype(jnp.bfloat16)
 
 
 def spread(metric):
     f32, bf = jnp.float32, jnp.bfloat16
-
-    def third(n):
-        return jnp.floor((n.astype(f32) + 0.5) * (1.0 / 3.0))
-
-    def iota(shape, dim):
-        return lax.broadcasted_iota(jnp.int32, shape, dim)
-
-    left = (third(iota((48, 16), 0)) == iota((48, 16), 1).astype(f32)).astype(f32).astype(bf)
-    right = (third(iota((128, CH), 1)) == iota((128, CH), 0).astype(f32)).astype(f32).astype(bf)
+    left = jnp.where(third(iota((CH, 128), 0)) == iota((CH, 128), 1), 1.0, 0.0).astype(bf)
+    right = jnp.where(third(iota((128, CH), 1)) == iota((128, CH), 0), 1.0, 0.0).astype(bf)
     rows = jnp.dot(left, metric, preferred_element_type=f32).astype(bf)
     wide = jnp.dot(rows, right, preferred_element_type=f32)
-    a, b = iota((48, CH), 0), iota((48, CH), 1)
-    same = (a.astype(f32) - 3.0 * third(a)) == (b.astype(f32) - 3.0 * third(b))
-    return jnp.where(same, wide, 0.0).astype(bf)
-
-
-def kernel(half, survive, metric, perm, out, block, kron, snd, rcv, m3, fb, ft, dvr, dv, cs1, csi1, rb1, rbi1, cs, csi, rb, rbi,
-           kbuf, s1f, s1n, r1f, r1n, s2f, s2n, r2f, r2n, s3, r3, s4, r4,
+    a, b = iota((CH, CH), 0), iota((CH, CH), 1)
+    return jnp.where(a - 3.0 * third(a) == b - 3.0 * third(b), wide, 0.0).astype(bf)
+
+
+def kernel(half, survive, metric, out, block, perm, whole, snd, rcv, m3, fb, ft, dvr, dv, cs1, csi1, rb1, rbi1, cs, csi, rb, rbi,
+           kbuf, s1f, s1n, r1f, r1n, s2f, s2n, r2f, r2n, s3, r3, fin, s4, r4,
            lds, p1s, p1r, ks, kr, fs, fr, d1s, d1r, ds_, dr,
            q1fs, q1fr, q1ns, q1nr, q2fs, q2fr, q2ns, q2nr, q3s, q3r, q4s, q4r):
     f32 = jnp.float32
@@ -89,13 +87,6 @@
         pl.semaphore_signal(bar, inc=1, device_id=ring1(o), device_id_type=MESH)
         pl.semaphore_signal(bar, inc=1, device_id=ring2(o), device_id_type=MESH)
 
-    kron[...] = spread(metric[...])
-
-    @pl.when(has_mirror)
-    def _():
-        for o, a in mirror:
-            pl.semaphore_signal(bar, inc=1, device_id=(a, o), device_id_type=MESH)
-
     def rcopy(src, dst, ss, rs, dev):
         return pltpu.make_async_remote_copy(src_ref=src, dst_ref=dst, send_sem=ss, recv_sem=rs,
                                             device_id=dev, device_id_type=MESH)
@@ -103,9 +94,9 @@
     def al48(v):
         return pl.ds(pl.multiple_of(v * 48, 16), 48)
 
-    def krcopy(o):
-        dst = m3.at[al48(aux)]
-        return rcopy(kron, dst, ks.at[o], kr.at[o], ((aux + o) % 8, orb))
+    def mcopy(o):
+        rows = pl.ds(pl.multiple_of(aux * 16, 16), 16)
+        return rcopy(metric, whole.at[rows], ks.at[o], kr.at[o], ((aux + o) % 8, orb))
 
     def send(q, o, flip):
         dev = 2 * ((z + o) % 4) + (c + flip) % 2
@@ -118,33 +109,33 @@
         flags = [jnp.full((1, 128), survive[0, 0, 3 * q + n].astype(f32)) for n in range(3)]
         return jnp.concatenate(flags, axis=1).astype(jnp.bfloat16)
 
-    @pl.loop(0, NCH)
-    def _(q):
+    def sort(q):
         load(q).wait()
         kept = block[q] * gate(q)
         snd[q] = jnp.dot(perm[...], kept, preferred_element_type=f32).astype(jnp.bfloat16)
         rcv[q, al48(aux), :] = snd[q, al48(aux), :]
 
-    @pl.when(has_mirror)
-    def _():
-        pl.semaphore_wait(bar, 15)
-
-    @pl.when(jnp.logical_not(has_mirror))
-    def _():
-        pl.semaphore_wait(bar, 13)
-
-    for o in range(1, 8):
-        krcopy(o).start()
-    m3[al48(aux), :] = kron[...]
-
-    @pl.loop(0, NCH)
-    def _(q):
+    def sends(q):
         for o, flip in ORDER:
             send(q, o, flip).start()
 
+    perm[...] = sorting()
+    sort(0)
+    pl.semaphore_wait(bar, 13)
     for o in range(1, 8):
-        src = (aux + 8 - o) % 8
-        rcopy(kron, m3.at[al48(src)], ks.at[o], kr.at[o], (sib, orb)).wait_recv()
+        mcopy(o).start()
+    sends(0)
+    whole[pl.ds(pl.multiple_of(aux * 16, 16), 16), :] = metric[...]
+
+    @pl.loop(1, NCH)
+    def _(q):
+        sort(q)
+        sends(q)
+
+    for o in range(1, 8):
+        rows = pl.ds(pl.multiple_of((aux + 8 - o) % 8 * 16, 16), 16)
+        rcopy(metric, whole.at[rows], ks.at[o], kr.at[o], (sib, orb)).wait_recv()
+    m3[...] = spread(whole[...])
 
     def fcopy(q):
         return rcopy(fb.at[q, pl.ds(0, CH)], fb.at[q, pl.ds(CH, CH)], fs.at[q], fr.at[q], (sib, orb))
@@ -208,16 +199,19 @@
         sc = cs[n, pl.ds(q, 1), :] * rb[n, h, pl.ds(p, 1), :]
         return val.astype(jnp.int32).astype(f32) * sc
 
+    def held(p, k):
+        return jnp.logical_or(k < 4, jnp.logical_and(k == 4, p % 2 == p // 4))
+
     def where(t, u, m):
         r = row_of(t, u)
         p = r // 2
-        k = (p + c) % 2 + 2 * m
-        return r % 2, p, (p + k) % 8, k + p // 4 <= 4
+        k = c + 2 * m
+        return r % 2, p, (p + k) % 8, held(p, k)
 
     tp, tm, tf = (me1 + 1) % 4, (me1 + 3) % 4, (me1 + 2) % 4
 
     def pair_of(k, j):
-        g = (k - j) // 5
+        g = (k - j + j % 2) // 5
         return j + g * (k - j), k - g * (k - j)
 
     def place(p, q, h):
@@ -230,7 +224,7 @@
         def _(j):
             p, q = pair_of(k, j)
 
-            @pl.when(q % 2 == c)
+            @pl.when((p + q) % 2 == c)
             def _():
                 body(p, q)
 
@@ -319,6 +313,10 @@
         fb[k, 0:CH, :] = jnp.dot(m3[...], rcv[k], preferred_element_type=f32).astype(jnp.bfloat16)
         fcopy(k).start()
 
+        @pl.when(k > 0)
+        def _():
+            compute(k - 1)
+
         @pl.when(k > 1)
         def _():
             norms(k - 2)
@@ -329,8 +327,8 @@
             collect(k - 3)
 
         pair(k)
-        compute(k)
-
+
+    compute(NCH - 1)
     norms(NCH - 2)
     norms(NCH - 1)
     gather(1, ring2)
@@ -396,8 +394,11 @@
     d2 = gathered(2, zline)
     tables(7, d2)
 
-    def last(m, o):
-        return rcopy(s3.at[m], r3.at[o - 1], q3s.at[m], q3r.at[o - 1], zdev(4 - o, c))
+    def last(m, o, q):
+        return rcopy(s3.at[m], r3.at[o], q3s.at[m], q3r.at[o], zdev(4 - o, q % 2))
+
+    def stays(o, q):
+        return jnp.logical_and(o == 0, q % 2 == c)
 
     @pl.loop(0, 3)
     def _(m):
@@ -405,13 +406,16 @@
             near2(m, 0).wait_recv()
             near2(m, 1).wait_recv()
             tile = tile + dec(r2n[0, m], 5, h, p, q) + dec(r2n[1, m], 6, h, p, q)
-            kbuf[0, me2 * 3 + m] = tile
             o = (z + 4 - q // 2) % 4
 
-            @pl.when(o > 0)
+            @pl.when(stays(o, q))
+            def _():
+                fin[...] = tile
+
+            @pl.when(jnp.logical_not(stays(o, q)))
             def _():
                 s3[m] = enc(tile, 7, h, p, q)
-                last(m, o).start()
+                last(m, o, q).start()
 
         own1(me2, m, then)
 
@@ -419,16 +423,19 @@
         return rcopy(s4.at[h], r4.at[orb % 2], q4s.at[h], q4r.at[orb % 2], (mirror[h][1], mirror[h][0]))
 
     kk = (aux + 8 - pr) % 8
-    owner = kk + pr // 4 <= 4
+    owner = held(pr, kk)
+
+    def got(o):
+        rcopy(s3.at[0], r3.at[o], q3s.at[0], q3r.at[o], zdev(o, c)).wait_recv()
+        return dec(r3[o], 7 + o, orb % 2, pr, aux)
 
     @pl.when(owner)
     def _():
-        h = orb % 2
-        m = kk // 2
-        tile = kbuf[0, me2 * 3 + m]
-        for o in range(1, 4):
-            rcopy(s3.at[0], r3.at[o - 1], q3s.at[0], q3r.at[o - 1], zdev(o, c)).wait_recv()
-            tile = tile + dec(r3[o - 1], 7 + o, h, pr, aux)
+        @pl.when(pr % 2 == 1)
+        def _():
+            fin[...] = got(0)
+
+        tile = fin[...] + got(1) + got(2) + got(3)
         out[...] = tile
 
         @pl.when(has_mirror)
@@ -455,7 +462,7 @@
         out[HR:TR, :] = jnp.concatenate([parts[0][:, TR:], parts[1][:, TR:]], axis=1)
 
     for o in range(1, 8):
-        krcopy(o).wait_send()
+        mcopy(o).wait_send()
 
     @pl.loop(0, NCH)
     def _(q):
@@ -498,9 +505,9 @@
         _, _, q, ok = where(me1, me2, m)
         o = (z + 4 - q // 2) % 4
 
-        @pl.when(jnp.logical_and(ok, o > 0))
-        def _():
-            last(m, o).wait_send()
+        @pl.when(jnp.logical_and(ok, jnp.logical_not(stays(o, q))))
+        def _():
+            last(m, o, q).wait_send()
 
     @pl.when(jnp.logical_and(owner, has_mirror))
     def _():
@@ -511,10 +518,9 @@
 def shards(half, metric, survive):
     bf, f32, i16 = jnp.bfloat16, jnp.float32, jnp.int16
     rows = half.reshape(CH, half.shape[-1])
-    perm = jnp.asarray(perm_matrix(), bf)
     vm, dma = pltpu.VMEM, pltpu.SemaphoreType.DMA
     scratch = [
-        vm((NCH, CH, CH), bf), vm((48, CH), bf),
+        vm((NCH, CH, CH), bf), vm((CH, CH), bf), vm((128, 128), bf),
         vm((NCH, CH, CH), bf), vm((NCH, CH, CH), bf), vm((CH, CH), bf),
         vm((NCH, 2 * CH, CH), bf), vm((NCH, CH, 2 * CH), bf),
         vm((4, NCH, 1, CH), f32), vm((12, 8, CH), f32),
@@ -523,24 +529,24 @@
         vm((3, 12, TR, CH), f32),
         vm((12, TR, CH), i16), vm((2, 12, TR, CH), i16), vm((2, 12, HR, CH), i16), vm((2, 12, TR, CH), i16),
         vm((3, TR, CH), i16), vm((2, 3, TR, CH), i16), vm((2, 3, HR, CH), i16), vm((2, 3, TR, CH), i16),
-        vm((3, TR, CH), i16), vm((3, TR, CH), i16),
+        vm((3, TR, CH), i16), vm((4, TR, CH), i16), vm((TR, CH), f32),
         vm((2, MR, CH), i16), vm((2, MR, CH), i16),
         dma((NCH,)), dma((NCH, 8)), dma((NCH, 8)), dma((8,)), dma((8,)), dma((NCH,)), dma((NCH,)),
         dma((4, NCH)), dma((4, NCH)), dma((12,)), dma((12,)),
         dma((12, 2)), dma((2, 12)), dma((2, 12)), dma((2, 12)),
         dma((3, 2)), dma((2, 3)), dma((2, 3)), dma((2, 3)),
-        dma((3,)), dma((3,)), dma((2,)), dma((2,)),
+        dma((3,)), dma((4,)), dma((2,)), dma((2,)),
     ]
     return pl.pallas_call(
         kernel,
         out_shape=jax.ShapeDtypeStruct((TR, CH), f32),
         in_specs=[pl.BlockSpec(memory_space=pl.ANY), pl.BlockSpec(memory_space=pltpu.SMEM),
-                  pl.BlockSpec(memory_space=pltpu.VMEM), pl.BlockSpec(memory_space=pltpu.VMEM)],
+                  pl.BlockSpec(memory_space=pltpu.VMEM)],
         out_specs=pl.BlockSpec(memory_space=pltpu.VMEM),
         scratch_shapes=scratch,
         compiler_params=pltpu.CompilerParams(collective_id=0, has_side_effects=True,
                                              vmem_limit_bytes=62 * 1024 * 1024),
-    )(rows, survive, metric, perm)
+    )(rows, survive, metric)
 
 
 def solution(mesh):

time: 110 us -> 107 us (0.973)
  Pallas kernels: 108 us -> 105 us
    pallas_call x1, Pallas kernels: 108 us -> 105 us  [shards(): pl.pallas_call(kernel, out_shape=jax.ShapeDtypeStruct((TR, CH), f32), in_...]
where the time goes in v5:
time: 107 us
  Pallas kernels  105 us (98%)
  local copies, waits for them, and re-layouts  1.69 us (2%)
    pallas_call x1, Pallas kernels, shards(): pl.pallas_call(kernel, out_shape=jax.ShapeDtypeStruct((TR, CH), f32), in_...  105 us

profile of v5, /device:TPU:96, one launch (start us, length us, event | category | flops | bytes accessed | tf_op | source)
XLA Modules:
  0.0 107.0 jit_solution(10711731285825813164)
XLA Ops:
  0.0 105.3 %shard_map.37 = f32[192,384]{1,0:T(8,128)} custom-call(bf16[384,3072]{1,0:T(8,128)(2,1)} %bitcast.1, s32[1,1,24]{2,1,0:T(1,128)} %survive.1, bf16[16,128]{1,0:T(8,128)(2,1)} %metric.1), custom_call_target="tpu_custom_call" | custom-call | tf_op jit(solution)/shard_map/pallas_call | solution.py:540
  105.3 1.7 %copy.5 = f32[192,384]{1,0:T(8,128)} copy(f32[192,384]{1,0:T(8,128)} %shard_map.37) | data formatting | bytes 589824

commit v6 on v5

--- a/solution.py
+++ b/solution.py
@@ -43,9 +43,8 @@
 
 
 def kernel(half, survive, metric, out, block, perm, whole, snd, rcv, m3, fb, ft, dvr, dv, cs1, csi1, rb1, rbi1, cs, csi, rb, rbi,
-           kbuf, s1f, s1n, r1f, r1n, s2f, s2n, r2f, r2n, s3, r3, fin, s4, r4,
-           lds, p1s, p1r, ks, kr, fs, fr, d1s, d1r, ds_, dr,
-           q1fs, q1fr, q1ns, q1nr, q2fs, q2fr, q2ns, q2nr, q3s, q3r, q4s, q4r):
+           kbuf, s1, r1, s2, r2, s3, r3, fin, s4, r4,
+           lds, p1s, p1r, ks, kr, fs, fr, d1s, d1r, ds_, dr, q1s, q1r, q2s, q2r, q3s, q3r, q4s, q4r):
     f32 = jnp.float32
     aux = lax.axis_index("aux")
     orb = lax.axis_index("orb")
@@ -177,9 +176,6 @@
             rcopy(dv.at[base], dv.at[base + o], ds_.at[base + o], dr.at[base + o], dev(o)).wait_recv()
         return [dv[base + o] for o in range(4)]
 
-    def ring_terms(d):
-        return [d[0], d[3], d[1], d[0] + d[3], d[0] + d[1], d[3] + d[2], d[1] + d[2]]
-
     def dcopy(q, o):
         return rcopy(dvr.at[0, q], dvr.at[4 - o, q], d1s.at[o, q], d1r.at[4 - o, q], ring1(o))
 
@@ -208,8 +204,6 @@
         k = c + 2 * m
         return r % 2, p, (p + k) % 8, held(p, k)
 
-    tp, tm, tf = (me1 + 1) % 4, (me1 + 3) % 4, (me1 + 2) % 4
-
     def pair_of(k, j):
         g = (k - j + j % 2) // 5
         return j + g * (k - j), k - g * (k - j)
@@ -228,14 +222,11 @@
             def _():
                 body(p, q)
 
-    def far1(i, half_at):
-        rows = pl.ds(half_at * HR, HR)
-        dst = 0 if half_at == 0 else 1
-        return rcopy(s1f.at[i, rows], r1f.at[dst, i], q1fs.at[i, half_at], q1fr.at[dst, i],
-                     ring1(1 if half_at == 0 else 3))
-
-    def near1(i, way, dev):
-        return rcopy(s1n.at[way, i], r1n.at[way, i], q1ns.at[way, i], q1nr.at[way, i], dev)
+    def tile1(role, i):
+        return rcopy(s1.at[role - 1, i], r1.at[3 - role, i], q1s.at[role - 1, i], q1r.at[3 - role, i], ring1(role))
+
+    def tile2(role, m):
+        return rcopy(s2.at[role - 1, m], r2.at[3 - role, m], q2s.at[role - 1, m], q2r.at[3 - role, m], ring2(role))
 
     def pair(k):
         fcopy(k).wait_recv()
@@ -255,15 +246,14 @@
                 i, role = place(p, q, h)
                 part = tile[h * TR:(h + 1) * TR]
 
-                @pl.when(role == 2)
+                @pl.when(role == 0)
                 def _():
-                    s1f[i] = enc1(part, 0, h, p, q)
-                    far1(i, 0).start()
-                    far1(i, 1).start()
-
-                @pl.when(role != 2)
+                    kbuf[i] = part
+
+                @pl.when(role > 0)
                 def _():
-                    kbuf[(role + 1) // 2, i] = part
+                    s1[role - 1, i] = enc1(part, 0, h, p, q)
+                    tile1(role, i).start()
 
         each(k, body)
 
@@ -271,40 +261,8 @@
         for o in range(1, 4):
             rcopy(dvr.at[0, k], dvr.at[o, k], d1s.at[o, k], d1r.at[o, k], ring1(o)).wait_recv()
         d = [dvr[o, k] for o in range(4)]
-        whole = d[0] + d[1] + d[2] + d[3]
-        tables1(k, slice(None), jnp.concatenate(ring_terms(d) + [whole], axis=0))
-        dv[4, pl.ds(k, 1), :] = whole
-
-    def pass_on(k):
-        def body(p, q):
-            for h in range(2):
-                i, role = place(p, q, h)
-
-                @pl.when(role % 2 == 1)
-                def _():
-                    way = role // 2
-                    pltpu.make_async_remote_copy(
-                        src_ref=s1f.at[i, pl.ds(0, HR)], dst_ref=r1f.at[way, i], send_sem=q1fs.at[i, 0],
-                        recv_sem=q1fr.at[way, i], device_id=ring1(1), device_id_type=MESH).wait_recv()
-                    rows = pl.ds(pl.multiple_of(way * HR, 32), HR)
-                    kbuf[1 + way, i, rows, :] = kbuf[1 + way, i, rows, :] + dec1(r1f[way, i], 1 + way, h, p, q)
-                    s1n[way, i] = enc1(kbuf[1 + way, i], 3 + way, h, p, q)
-                    near1(i, way, ring1(role)).start()
-
-        each(k, body)
-
-    def collect(k):
-        def body(p, q):
-            for h in range(2):
-                i, role = place(p, q, h)
-
-                @pl.when(role == 0)
-                def _():
-                    near1(i, 0, ring1(1)).wait_recv()
-                    near1(i, 1, ring1(1)).wait_recv()
-                    kbuf[0, i] = kbuf[0, i] + dec1(r1n[0, i], 5, h, p, q) + dec1(r1n[1, i], 6, h, p, q)
-
-        each(k, body)
+        tables1(k, slice(None), jnp.concatenate(d + d, axis=0))
+        dv[4, pl.ds(k, 1), :] = d[0] + d[1] + d[2] + d[3]
 
     @pl.loop(0, NCH)
     def _(k):
@@ -317,82 +275,54 @@
         def _():
             compute(k - 1)
 
-        @pl.when(k > 1)
-        def _():
-            norms(k - 2)
-            pass_on(k - 2)
-
-        @pl.when(k > 2)
-        def _():
-            collect(k - 3)
-
         pair(k)
 
     compute(NCH - 1)
-    norms(NCH - 2)
-    norms(NCH - 1)
+
+    @pl.loop(0, NCH)
+    def _(k):
+        norms(k)
+
     gather(1, ring2)
-    pass_on(NCH - 2)
-    collect(NCH - 3)
-    pass_on(NCH - 1)
-    collect(NCH - 2)
+
+    def total1(u, m, then):
+        h, p, q, ok = where(me1, u, m)
+        i = u * 3 + m
+
+        @pl.when(ok)
+        def _():
+            tile = kbuf[i]
+            for o in range(1, 4):
+                rcopy(s1.at[0, i], r1.at[o - 1, i], q1s.at[0, i], q1r.at[o - 1, i], ring1(1)).wait_recv()
+                tile = tile + dec1(r1[o - 1, i], o, h, p, q)
+            then(tile, h, p, q)
+
     d1 = gathered(1, ring2)
-    tables(0, ring_terms(d1))
+    tables(0, d1)
     dv[8] = d1[0] + d1[1] + d1[2] + d1[3]
 
     def zline(o):
         return zdev(o, c)
 
     gather(2, zline)
-    collect(NCH - 1)
-
-    def own1(u, m, then):
-        h, p, q, ok = where(me1, u, m)
-
-        @pl.when(ok)
-        def _():
-            then(kbuf[0, u * 3 + m], h, p, q)
-
-    def far2(m, half_at):
-        rows = pl.ds(half_at * HR, HR)
-        dst = 0 if half_at == 0 else 1
-        return rcopy(s2f.at[m, rows], r2f.at[dst, m], q2fs.at[m, half_at], q2fr.at[dst, m],
-                     ring2(1 if half_at == 0 else 3))
-
-    def near2(m, way):
-        return rcopy(s2n.at[way, m], r2n.at[way, m], q2ns.at[way, m], q2nr.at[way, m],
-                     ring2(1 if way == 0 else 3))
-
-    uf, up, um = (me2 + 2) % 4, (me2 + 1) % 4, (me2 + 3) % 4
+    for role in (2, 1, 3):
+        @pl.loop(0, 3)
+        def _(m):
+            def then(tile, h, p, q):
+                s2[role - 1, m] = enc(tile, 0, h, p, q)
+                tile2(role, m).start()
+
+            total1((me2 + role) % 4, m, then)
 
     @pl.loop(0, 3)
     def _(m):
         def then(tile, h, p, q):
-            s2f[m] = enc(tile, 0, h, p, q)
-            far2(m, 0).start()
-            far2(m, 1).start()
-
-        own1(uf, m, then)
-
-    for way, u in ((0, up), (1, um)):
-        @pl.loop(0, 3)
-        def _(m):
-            def then(tile, h, p, q):
-                far2(m, way).wait_recv()
-                add = dec(r2f[way, m], 1 + way, h, p, q)
-                low, high = tile[:HR], tile[HR:]
-                if way == 0:
-                    low = low + add
-                else:
-                    high = high + add
-                s2n[way, m, 0:HR, :] = enc(low, 3 + way, h, p, q)
-                s2n[way, m, HR:TR, :] = enc(high, 3 + way, h, p, q)
-                near2(m, way).start()
-
-            own1(u, m, then)
+            kbuf[m] = tile
+
+        total1(me2, m, then)
 
     d2 = gathered(2, zline)
-    tables(7, d2)
+    tables(4, d2)
 
     def last(m, o, q):
         return rcopy(s3.at[m], r3.at[o], q3s.at[m], q3r.at[o], zdev(4 - o, q % 2))
@@ -402,10 +332,14 @@
 
     @pl.loop(0, 3)
     def _(m):
-        def then(tile, h, p, q):
-            near2(m, 0).wait_recv()
-            near2(m, 1).wait_recv()
-            tile = tile + dec(r2n[0, m], 5, h, p, q) + dec(r2n[1, m], 6, h, p, q)
+        h, p, q, ok = where(me1, me2, m)
+
+        @pl.when(ok)
+        def _():
+            tile = kbuf[m]
+            for n in range(1, 4):
+                rcopy(s2.at[0, m], r2.at[n - 1, m], q2s.at[0, m], q2r.at[n - 1, m], ring2(1)).wait_recv()
+                tile = tile + dec(r2[n - 1, m], n, h, p, q)
             o = (z + 4 - q // 2) % 4
 
             @pl.when(stays(o, q))
@@ -414,10 +348,8 @@
 
             @pl.when(jnp.logical_not(stays(o, q)))
             def _():
-                s3[m] = enc(tile, 7, h, p, q)
+                s3[m] = enc(tile, 4, h, p, q)
                 last(m, o, q).start()
-
-        own1(me2, m, then)
 
     def mir(h):
         return rcopy(s4.at[h], r4.at[orb % 2], q4s.at[h], q4r.at[orb % 2], (mirror[h][1], mirror[h][0]))
@@ -427,7 +359,7 @@
 
     def got(o):
         rcopy(s3.at[0], r3.at[o], q3s.at[0], q3r.at[o], zdev(o, c)).wait_recv()
-        return dec(r3[o], 7 + o, orb % 2, pr, aux)
+        return dec(r3[o], 4 + o, orb % 2, pr, aux)
 
     @pl.when(owner)
     def _():
@@ -476,32 +408,21 @@
         for o in range(1, 4):
             rcopy(dv.at[4 * level], dv.at[4 * level], ds_.at[4 * level + o], dr.at[4 * level], dev(o)).wait_send()
 
-    @pl.loop(0, 12)
-    def _(j):
-        u, m = j // 3, j % 3
-
-        @pl.when(where(tf, u, m)[3])
-        def _():
-            far1(j, 0).wait_send()
-            far1(j, 1).wait_send()
-
-        for way, t in ((0, tp), (1, tm)):
-            @pl.when(where(t, u, m)[3])
+    for role in range(1, 4):
+        @pl.loop(0, 12)
+        def _(j):
+            @pl.when(where((me1 + role) % 4, j // 3, j % 3)[3])
             def _():
-                near1(j, way, ring1(1)).wait_send()
+                tile1(role, j).wait_send()
+
+        @pl.loop(0, 3)
+        def _(m):
+            @pl.when(where(me1, (me2 + role) % 4, m)[3])
+            def _():
+                tile2(role, m).wait_send()
 
     @pl.loop(0, 3)
     def _(m):
-        @pl.when(where(me1, uf, m)[3])
-        def _():
-            far2(m, 0).wait_send()
-            far2(m, 1).wait_send()
-
-        for way, u in ((0, up), (1, um)):
-            @pl.when(where(me1, u, m)[3])
-            def _():
-                near2(m, way).wait_send()
-
         _, _, q, ok = where(me1, me2, m)
         o = (z + 4 - q // 2) % 4
 
@@ -525,16 +446,14 @@
         vm((NCH, 2 * CH, CH), bf), vm((NCH, CH, 2 * CH), bf),
         vm((4, NCH, 1, CH), f32), vm((12, 8, CH), f32),
         vm((NCH, 8, CH), f32), vm((NCH, 8, CH), f32), vm((2, NCH, 8, CH), f32), vm((2, NCH, 8, CH), f32),
-        vm((11, 8, CH), f32), vm((11, 8, CH), f32), vm((11, 2, 8, CH), f32), vm((11, 2, 8, CH), f32),
-        vm((3, 12, TR, CH), f32),
-        vm((12, TR, CH), i16), vm((2, 12, TR, CH), i16), vm((2, 12, HR, CH), i16), vm((2, 12, TR, CH), i16),
-        vm((3, TR, CH), i16), vm((2, 3, TR, CH), i16), vm((2, 3, HR, CH), i16), vm((2, 3, TR, CH), i16),
+        vm((8, 8, CH), f32), vm((8, 8, CH), f32), vm((8, 2, 8, CH), f32), vm((8, 2, 8, CH), f32),
+        vm((12, TR, CH), f32), vm((3, 12, TR, CH), i16), vm((3, 12, TR, CH), i16),
+        vm((3, 3, TR, CH), i16), vm((3, 3, TR, CH), i16),
         vm((3, TR, CH), i16), vm((4, TR, CH), i16), vm((TR, CH), f32),
         vm((2, MR, CH), i16), vm((2, MR, CH), i16),
         dma((NCH,)), dma((NCH, 8)), dma((NCH, 8)), dma((8,)), dma((8,)), dma((NCH,)), dma((NCH,)),
         dma((4, NCH)), dma((4, NCH)), dma((12,)), dma((12,)),
-        dma((12, 2)), dma((2, 12)), dma((2, 12)), dma((2, 12)),
-        dma((3, 2)), dma((2, 3)), dma((2, 3)), dma((2, 3)),
+        dma((3, 12)), dma((3, 12)), dma((3, 3)), dma((3, 3)),
         dma((3,)), dma((4,)), dma((2,)), dma((2,)),
     ]
     return pl.pallas_call(

time: 107 us -> 104 us (0.972)
  the two profiles are of different devices: /device:TPU:96 before, /device:TPU:123 now
where the time goes in v6:
time: 104 us
  Pallas kernels  103 us (99%)
  local copies, waits for them, and re-layouts  1.69 us (2%)
    pallas_call x1, Pallas kernels, shards(): pl.pallas_call(kernel, out_shape=jax.ShapeDtypeStruct((TR, CH), f32), in_...  103 us

profile of v6, /device:TPU:123, one launch (start us, length us, event | category | flops | bytes accessed | tf_op | source)
XLA Modules:
  0.0 104.2 jit_solution(2024684328498962153)
XLA Ops:
  0.0 102.5 %shard_map.37 = f32[192,384]{1,0:T(8,128)} custom-call(bf16[384,3072]{1,0:T(8,128)(2,1)} %bitcast.1, s32[1,1,24]{2,1,0:T(1,128)} %survive.1, bf16[16,128]{1,0:T(8,128)(2,1)} %metric.1), custom_call_target="tpu_custom_call" | custom-call | tf_op jit(solution)/shard_map/pallas_call | solution.py:459
  102.5 1.7 %copy.5 = f32[192,384]{1,0:T(8,128)} copy(f32[192,384]{1,0:T(8,128)} %shard_map.37) | data formatting | bytes 589824

commit v7 on v6

--- a/solution.py
+++ b/solution.py
@@ -10,7 +10,6 @@
 NCH = 8
 TR = 192
 HR = 96
-MR = 112
 TOP = 32700.0
 TINY = 1e-36
 ORDER = ((2, 0), (2, 1), (1, 0), (3, 0), (1, 1), (3, 1), (0, 1))
@@ -43,7 +42,7 @@
 
 
 def kernel(half, survive, metric, out, block, perm, whole, snd, rcv, m3, fb, ft, dvr, dv, cs1, csi1, rb1, rbi1, cs, csi, rb, rbi,
-           kbuf, s1, r1, s2, r2, s3, r3, fin, s4, r4,
+           kbuf, s1, r1, s2, r2, s3, r3, s4, r4,
            lds, p1s, p1r, ks, kr, fs, fr, d1s, d1r, ds_, dr, q1s, q1r, q2s, q2r, q3s, q3r, q4s, q4r):
     f32 = jnp.float32
     aux = lax.axis_index("aux")
@@ -67,9 +66,6 @@
         return (2 * ((z + o) % 4) + core, orb)
 
     pr = orb // 2
-    mirror = [(2 * aux + h, pr) for h in range(2)]
-    has_mirror = aux != pr
-
     def cut(q):
         return pl.ds(pl.multiple_of(q * CH, 128), CH)
 
@@ -195,32 +191,28 @@
         sc = cs[n, pl.ds(q, 1), :] * rb[n, h, pl.ds(p, 1), :]
         return val.astype(jnp.int32).astype(f32) * sc
 
-    def held(p, k):
-        return jnp.logical_or(k < 4, jnp.logical_and(k == 4, p % 2 == p // 4))
-
-    def where(t, u, m):
-        r = row_of(t, u)
-        p = r // 2
-        k = c + 2 * m
-        return r % 2, p, (p + k) % 8, held(p, k)
-
-    def pair_of(k, j):
-        g = (k - j + j % 2) // 5
-        return j + g * (k - j), k - g * (k - j)
+    def where(t, i):
+        p = 2 * (i // 4) + t // 2
+        q = 2 * (i % 4) + (i // 4 + c) % 2
+        return t % 2, p, q, q >= p
+
+    def slot(u, m):
+        return m * 4 + (u - m + 4) % 4
+
+    def source(p, q, h):
+        core = (p // 2 + q) % 2
+        t, u = 2 * (p % 2) + h, (p // 2 + q // 2) % 4
+        return t * (4 - 3 * core) + u * (1 + 3 * core), core
 
     def place(p, q, h):
-        a, b = p // 2, 2 * (p % 2) + h
-        t, u = a * (1 - c) + b * c, b * (1 - c) + a * c
-        return u * 3 + ((q - p + 8) % 8) // 2, (t - me1 + 4) % 4
+        return (p // 2) * 4 + q // 2, (2 * (p % 2) + h - me1 + 4) % 4
 
     def each(k, body):
         @pl.loop(0, k + 1)
         def _(j):
-            p, q = pair_of(k, j)
-
-            @pl.when((p + q) % 2 == c)
-            def _():
-                body(p, q)
+            @pl.when((j // 2 + k) % 2 == c)
+            def _():
+                body(j, k)
 
     def tile1(role, i):
         return rcopy(s1.at[role - 1, i], r1.at[3 - role, i], q1s.at[role - 1, i], q1r.at[3 - role, i], ring1(role))
@@ -286,8 +278,8 @@
     gather(1, ring2)
 
     def total1(u, m, then):
-        h, p, q, ok = where(me1, u, m)
-        i = u * 3 + m
+        i = slot(u, m)
+        h, p, q, ok = where(me1, i)
 
         @pl.when(ok)
         def _():
@@ -306,7 +298,7 @@
 
     gather(2, zline)
     for role in (2, 1, 3):
-        @pl.loop(0, 3)
+        @pl.loop(0, 4)
         def _(m):
             def then(tile, h, p, q):
                 s2[role - 1, m] = enc(tile, 0, h, p, q)
@@ -314,7 +306,7 @@
 
             total1((me2 + role) % 4, m, then)
 
-    @pl.loop(0, 3)
+    @pl.loop(0, 4)
     def _(m):
         def then(tile, h, p, q):
             kbuf[m] = tile
@@ -324,15 +316,18 @@
     d2 = gathered(2, zline)
     tables(4, d2)
 
-    def last(m, o, q):
-        return rcopy(s3.at[m], r3.at[o], q3s.at[m], q3r.at[o], zdev(4 - o, q % 2))
-
-    def stays(o, q):
-        return jnp.logical_and(o == 0, q % 2 == c)
-
-    @pl.loop(0, 3)
+    def last(m, h, p, q):
+        return rcopy(s3.at[m], r3.at[z], q3s.at[m], q3r.at[z], (q, 2 * p + h))
+
+    def turned(m, n, h, p, q):
+        return rcopy(s4.at[m, n], r4.at[h, z], q4s.at[m, n], q4r.at[h, z], (p, 2 * q + n))
+
+    def this(a, o):
+        return jnp.logical_and(aux == a, orb == o)
+
+    @pl.loop(0, 4)
     def _(m):
-        h, p, q, ok = where(me1, me2, m)
+        h, p, q, ok = where(me1, slot(me2, m))
 
         @pl.when(ok)
         def _():
@@ -340,58 +335,72 @@
             for n in range(1, 4):
                 rcopy(s2.at[0, m], r2.at[n - 1, m], q2s.at[0, m], q2r.at[n - 1, m], ring2(1)).wait_recv()
                 tile = tile + dec(r2[n - 1, m], n, h, p, q)
-            o = (z + 4 - q // 2) % 4
-
-            @pl.when(stays(o, q))
-            def _():
-                fin[...] = tile
-
-            @pl.when(jnp.logical_not(stays(o, q)))
-            def _():
-                s3[m] = enc(tile, 4, h, p, q)
-                last(m, o, q).start()
-
-    def mir(h):
-        return rcopy(s4.at[h], r4.at[orb % 2], q4s.at[h], q4r.at[orb % 2], (mirror[h][1], mirror[h][0]))
-
-    kk = (aux + 8 - pr) % 8
-    owner = held(pr, kk)
-
-    def got(o):
-        rcopy(s3.at[0], r3.at[o], q3s.at[0], q3r.at[o], zdev(o, c)).wait_recv()
-        return dec(r3[o], 4 + o, orb % 2, pr, aux)
-
-    @pl.when(owner)
+            code = jnp.round(tile * (csi[4, pl.ds(q, 1), :] * rbi[4, h, pl.ds(p, 1), :]))
+            full = code.astype(jnp.int32).astype(jnp.int16)
+
+            @pl.when(this(q, 2 * p + h))
+            def _():
+                r3[z] = full
+
+            @pl.when(jnp.logical_not(this(q, 2 * p + h)))
+            def _():
+                s3[m] = full
+                last(m, h, p, q).start()
+
+            @pl.when(q > p)
+            def _():
+                for n in range(2):
+                    part = code[:, n * TR:(n + 1) * TR]
+                    flat = jnp.concatenate([part[:HR], part[HR:]], axis=1).astype(jnp.int32).astype(jnp.int16)
+
+                    @pl.when(this(p, 2 * q + n))
+                    def _():
+                        r4[h, z] = flat
+
+                    @pl.when(jnp.logical_not(this(p, 2 * q + n)))
+                    def _():
+                        s4[m, n] = flat
+                        turned(m, n, h, p, q).start()
+
+    def other(p, q, h, level):
+        src, core = source(p, q, h)
+        return jnp.logical_not(this(2 * level + core, src))
+
+    @pl.when(aux >= pr)
     def _():
-        @pl.when(pr % 2 == 1)
-        def _():
-            fin[...] = got(0)
-
-        tile = fin[...] + got(1) + got(2) + got(3)
+        h = orb % 2
+        for o in range(4):
+            up = (z + o) % 4
+
+            @pl.when(other(pr, aux, h, up))
+            def _():
+                rcopy(s3.at[0], r3.at[up], q3s.at[0], q3r.at[up], (sib, orb)).wait_recv()
+        tile = dec(r3[z], 4, h, pr, aux)
+        for o in range(1, 4):
+            tile = tile + dec(r3[(z + o) % 4], 4 + o, h, pr, aux)
         out[...] = tile
 
-        @pl.when(has_mirror)
-        def _():
-            turned = tile.T
-            for h2 in range(2):
-                part = turned[h2 * TR:(h2 + 1) * TR]
-                flat = jnp.concatenate([part[:HR], part[HR:]], axis=1)
-                top = jnp.max(jnp.abs(flat), axis=0, keepdims=True)
-                power = jnp.ceil(jnp.log2(jnp.maximum(top, TINY)))
-                s4[h2, 0:HR, :] = jnp.round(flat * (jnp.exp2(-power) * TOP)).astype(jnp.int32).astype(jnp.int16)
-                s4[h2, HR:MR, :] = jnp.broadcast_to(power, (16, CH)).astype(jnp.int32).astype(jnp.int16)
-                mir(h2).start()
-
-    @pl.when(jnp.logical_not(owner))
+    @pl.when(aux < pr)
     def _():
-        for h2 in range(2):
-            rcopy(s4.at[0], r4.at[h2], q4s.at[0], q4r.at[h2], (mirror[h2][1], mirror[h2][0])).wait_recv()
-        parts = []
-        for h2 in range(2):
-            power = r4[h2, HR:MR, :].astype(jnp.int32).astype(f32)[0:1]
-            parts.append(r4[h2, 0:HR, :].astype(jnp.int32).astype(f32) * (jnp.exp2(power) * (1.0 / TOP)))
-        out[0:HR, :] = jnp.concatenate([parts[0][:, :TR], parts[1][:, :TR]], axis=1)
-        out[HR:TR, :] = jnp.concatenate([parts[0][:, TR:], parts[1][:, TR:]], axis=1)
+        n = orb % 2
+        for h in range(2):
+            for o in range(4):
+                up = (z + o) % 4
+
+                @pl.when(other(aux, pr, h, up))
+                def _():
+                    rcopy(s4.at[0, 0], r4.at[h, up], q4s.at[0, 0], q4r.at[h, up], (sib, orb)).wait_recv()
+        wide = []
+        for h in range(2):
+            flat = jnp.zeros((HR, CH), f32)
+            for o in range(4):
+                sc = cs[4 + o, pl.ds(pr, 1), :]
+                low = jnp.concatenate([sc[:, :TR], sc[:, :TR]], axis=1)
+                high = jnp.concatenate([sc[:, TR:], sc[:, TR:]], axis=1)
+                sc = jnp.where(n == 0, low, high) * rb[4 + o, h, pl.ds(aux, 1), :]
+                flat = flat + r4[h, (z + o) % 4].astype(jnp.int32).astype(f32) * sc
+            wide.append(jnp.concatenate([flat[:, :TR], flat[:, TR:]], axis=0).T)
+        out[...] = jnp.concatenate(wide, axis=1)
 
     for o in range(1, 8):
         mcopy(o).wait_send()
@@ -409,31 +418,30 @@
             rcopy(dv.at[4 * level], dv.at[4 * level], ds_.at[4 * level + o], dr.at[4 * level], dev(o)).wait_send()
 
     for role in range(1, 4):
-        @pl.loop(0, 12)
-        def _(j):
-            @pl.when(where((me1 + role) % 4, j // 3, j % 3)[3])
-            def _():
-                tile1(role, j).wait_send()
-
-        @pl.loop(0, 3)
+        @pl.loop(0, 16)
+        def _(i):
+            @pl.when(where((me1 + role) % 4, i)[3])
+            def _():
+                tile1(role, i).wait_send()
+
+        @pl.loop(0, 4)
         def _(m):
-            @pl.when(where(me1, (me2 + role) % 4, m)[3])
+            @pl.when(where(me1, slot((me2 + role) % 4, m))[3])
             def _():
                 tile2(role, m).wait_send()
 
-    @pl.loop(0, 3)
+    @pl.loop(0, 4)
     def _(m):
-        _, _, q, ok = where(me1, me2, m)
-        o = (z + 4 - q // 2) % 4
-
-        @pl.when(jnp.logical_and(ok, jnp.logical_not(stays(o, q))))
+        h, p, q, ok = where(me1, slot(me2, m))
+
+        @pl.when(jnp.logical_and(ok, jnp.logical_not(this(q, 2 * p + h))))
         def _():
-            last(m, o, q).wait_send()
-
-    @pl.when(jnp.logical_and(owner, has_mirror))
-    def _():
-        for h2 in range(2):
-            mir(h2).wait_send()
+            last(m, h, p, q).wait_send()
+
+        for n in range(2):
+            @pl.when(jnp.logical_and(jnp.logical_and(ok, q > p), jnp.logical_not(this(p, 2 * q + n))))
+            def _():
+                turned(m, n, h, p, q).wait_send()
 
 
 def shards(half, metric, survive):
@@ -447,14 +455,13 @@
         vm((4, NCH, 1, CH), f32), vm((12, 8, CH), f32),
         vm((NCH, 8, CH), f32), vm((NCH, 8, CH), f32), vm((2, NCH, 8, CH), f32), vm((2, NCH, 8, CH), f32),
         vm((8, 8, CH), f32), vm((8, 8, CH), f32), vm((8, 2, 8, CH), f32), vm((8, 2, 8, CH), f32),
-        vm((12, TR, CH), f32), vm((3, 12, TR, CH), i16), vm((3, 12, TR, CH), i16),
-        vm((3, 3, TR, CH), i16), vm((3, 3, TR, CH), i16),
-        vm((3, TR, CH), i16), vm((4, TR, CH), i16), vm((TR, CH), f32),
-        vm((2, MR, CH), i16), vm((2, MR, CH), i16),
+        vm((16, TR, CH), f32), vm((3, 16, TR, CH), i16), vm((3, 16, TR, CH), i16),
+        vm((3, 4, TR, CH), i16), vm((3, 4, TR, CH), i16),
+        vm((4, TR, CH), i16), vm((4, TR, CH), i16), vm((4, 2, HR, CH), i16), vm((2, 4, HR, CH), i16),
         dma((NCH,)), dma((NCH, 8)), dma((NCH, 8)), dma((8,)), dma((8,)), dma((NCH,)), dma((NCH,)),
         dma((4, NCH)), dma((4, NCH)), dma((12,)), dma((12,)),
-        dma((3, 12)), dma((3, 12)), dma((3, 3)), dma((3, 3)),
-        dma((3,)), dma((4,)), dma((2,)), dma((2,)),
+        dma((3, 16)), dma((3, 16)), dma((3, 4)), dma((3, 4)),
+        dma((4,)), dma((4,)), dma((4, 2)), dma((2, 4)),
     ]
     return pl.pallas_call(
         kernel,

time: 104 us -> 86 us (0.83)
  the two profiles are of different devices: /device:TPU:123 before, /device:TPU:103 now
where the time goes in v7:
time: 86 us; the launch traced here: 85.8 us
  Pallas kernels  84.1 us (98%)
  local copies, waits for them, and re-layouts  1.69 us (2%)
    pallas_call x1, Pallas kernels, shards(): pl.pallas_call(kernel, out_shape=jax.ShapeDtypeStruct((TR, CH), f32), in_...  84.1 us

profile of v7, /device:TPU:103, one launch (start us, length us, event | category | flops | bytes accessed | tf_op | source)
XLA Modules:
  0.0 85.8 jit_solution(10744016016329644650)
XLA Ops:
  0.0 84.1 %shard_map.37 = f32[192,384]{1,0:T(8,128)} custom-call(bf16[384,3072]{1,0:T(8,128)(2,1)} %bitcast.1, s32[1,1,24]{2,1,0:T(1,128)} %survive.1, bf16[16,128]{1,0:T(8,128)(2,1)} %metric.1), custom_call_target="tpu_custom_call" | custom-call | tf_op jit(solution)/shard_map/pallas_call | solution.py:466
  84.1 1.7 %copy.5 = f32[192,384]{1,0:T(8,128)} copy(f32[192,384]{1,0:T(8,128)} %shard_map.37) | data formatting | bytes 589824

commit v8 on v7

--- a/solution.py
+++ b/solution.py
@@ -62,6 +62,9 @@
     def ring2(o):
         return (aux, row_of(me1, (me2 + o) % 4))
 
+    def cross(o):
+        return (sib, row_of(me1, (me2 + o) % 4))
+
     def zdev(o, core):
         return (2 * ((z + o) % 4) + core, orb)
 
@@ -81,6 +84,7 @@
     for o in range(1, 4):
         pl.semaphore_signal(bar, inc=1, device_id=ring1(o), device_id_type=MESH)
         pl.semaphore_signal(bar, inc=1, device_id=ring2(o), device_id_type=MESH)
+        pl.semaphore_signal(bar, inc=1, device_id=cross(o), device_id_type=MESH)
 
     def rcopy(src, dst, ss, rs, dev):
         return pltpu.make_async_remote_copy(src_ref=src, dst_ref=dst, send_sem=ss, recv_sem=rs,
@@ -116,7 +120,7 @@
 
     perm[...] = sorting()
     sort(0)
-    pl.semaphore_wait(bar, 13)
+    pl.semaphore_wait(bar, 16)
     for o in range(1, 8):
         mcopy(o).start()
     sends(0)
@@ -173,7 +177,7 @@
         return [dv[base + o] for o in range(4)]
 
     def dcopy(q, o):
-        return rcopy(dvr.at[0, q], dvr.at[4 - o, q], d1s.at[o, q], d1r.at[4 - o, q], ring1(o))
+        return rcopy(dvr.at[0, q], dvr.at[4 - o, q], d1s.at[o, q], d1r.at[4 - o, q], cross(o))
 
     def enc1(val, n, h, p, q):
         inv = csi1[q, pl.ds(n, 1), :] * rbi1[h, p, pl.ds(n, 1), :]
@@ -225,7 +229,8 @@
         both = fb[k]
         ft[k] = both.T
         wide = both.astype(f32)
-        norm = jnp.sum(wide * wide, axis=0, keepdims=True)
+        wide = wide * wide
+        norm = jnp.sum(wide[:CH], axis=0, keepdims=True) + jnp.sum(wide[CH:], axis=0, keepdims=True)
         dvr[0, k] = norm
         for o in range(1, 4):
             dcopy(k, o).start()
@@ -267,19 +272,35 @@
         def _():
             compute(k - 1)
 
+        @pl.when(k > 3)
+        def _():
+            norms(k - 4)
+
         pair(k)
 
     compute(NCH - 1)
 
-    @pl.loop(0, NCH)
+    @pl.loop(NCH - 4, NCH)
     def _(k):
         norms(k)
 
     gather(1, ring2)
 
-    def total1(u, m, then):
-        i = slot(u, m)
+    d1 = gathered(1, ring2)
+    tables(0, d1)
+    dv[8] = d1[0] + d1[1] + d1[2] + d1[3]
+
+    def zline(o):
+        return zdev(o, c)
+
+    gather(2, zline)
+    @pl.loop(0, 16)
+    def _(n):
+        b = n // 4
+        a = 2 * (n % 2) + (n % 4 // 2) * (1 - 2 * c) + c
+        i = a * 4 + b
         h, p, q, ok = where(me1, i)
+        role = (a + b - me2 + 4) % 4
 
         @pl.when(ok)
         def _():
@@ -287,31 +308,15 @@
             for o in range(1, 4):
                 rcopy(s1.at[0, i], r1.at[o - 1, i], q1s.at[0, i], q1r.at[o - 1, i], ring1(1)).wait_recv()
                 tile = tile + dec1(r1[o - 1, i], o, h, p, q)
-            then(tile, h, p, q)
-
-    d1 = gathered(1, ring2)
-    tables(0, d1)
-    dv[8] = d1[0] + d1[1] + d1[2] + d1[3]
-
-    def zline(o):
-        return zdev(o, c)
-
-    gather(2, zline)
-    for role in (2, 1, 3):
-        @pl.loop(0, 4)
-        def _(m):
-            def then(tile, h, p, q):
-                s2[role - 1, m] = enc(tile, 0, h, p, q)
-                tile2(role, m).start()
-
-            total1((me2 + role) % 4, m, then)
-
-    @pl.loop(0, 4)
-    def _(m):
-        def then(tile, h, p, q):
-            kbuf[m] = tile
-
-        total1(me2, m, then)
+
+            @pl.when(role == 0)
+            def _():
+                kbuf[i] = tile
+
+            @pl.when(role > 0)
+            def _():
+                s2[role - 1, a] = enc(tile, 0, h, p, q)
+                tile2(role, a).start()
 
     d2 = gathered(2, zline)
     tables(4, d2)
@@ -326,12 +331,14 @@
         return jnp.logical_and(aux == a, orb == o)
 
     @pl.loop(0, 4)
-    def _(m):
-        h, p, q, ok = where(me1, slot(me2, m))
+    def _(b):
+        m = (me2 - b + 4) % 4
+        i = m * 4 + b
+        h, p, q, ok = where(me1, i)
 
         @pl.when(ok)
         def _():
-            tile = kbuf[m]
+            tile = kbuf[i]
             for n in range(1, 4):
                 rcopy(s2.at[0, m], r2.at[n - 1, m], q2s.at[0, m], q2r.at[n - 1, m], ring2(1)).wait_recv()
                 tile = tile + dec(r2[n - 1, m], n, h, p, q)

time: 86 us -> 86.7 us (level)
  the two profiles are of different devices: /device:TPU:103 before, /device:TPU:4 now
where the time goes in v8:
time: 86.7 us; the launch traced here: 86.5 us
  Pallas kernels  84.8 us (98%)
  local copies, waits for them, and re-layouts  1.69 us (2%)
    pallas_call x1, Pallas kernels, shards(): pl.pallas_call(kernel, out_shape=jax.ShapeDtypeStruct((TR, CH), f32), in_...  84.8 us

profile of v8, /device:TPU:4, one launch (start us, length us, event | category | flops | bytes accessed | tf_op | source)
XLA Modules:
  0.0 86.5 jit_solution(1611324448028627050)
XLA Ops:
  0.0 84.8 %shard_map.37 = f32[192,384]{1,0:T(8,128)} custom-call(bf16[384,3072]{1,0:T(8,128)(2,1)} %bitcast.1, s32[1,1,24]{2,1,0:T(1,128)} %survive.1, bf16[16,128]{1,0:T(8,128)(2,1)} %metric.1), custom_call_target="tpu_custom_call" | custom-call | tf_op jit(solution)/shard_map/pallas_call | solution.py:473
  84.8 1.7 %copy.5 = f32[192,384]{1,0:T(8,128)} copy(f32[192,384]{1,0:T(8,128)} %shard_map.37) | data formatting | bytes 589824

commit v9 on v8

--- a/solution.py
+++ b/solution.py
@@ -69,11 +69,17 @@
         return (2 * ((z + o) % 4) + core, orb)
 
     pr = orb // 2
+    def block_at(s):
+        return (2 * s) % 8 + s // 4
+
+    def turn_of(v):
+        return v // 2 + 4 * (v % 2)
+
     def cut(q):
         return pl.ds(pl.multiple_of(q * CH, 128), CH)
 
     def load(q):
-        return pltpu.make_async_copy(half.at[:, cut(q)], block.at[q], lds.at[q])
+        return pltpu.make_async_copy(half.at[:, cut(block_at(q))], block.at[q], lds.at[q])
 
     for q in range(NCH):
         load(q).start()
@@ -105,7 +111,7 @@
         return rcopy(rcv.at[q, al48(a)], rcv.at[q, al48(a)], p1s.at[q, 0], p1r.at[q, a], (sib, orb))
 
     def gate(q):
-        flags = [jnp.full((1, 128), survive[0, 0, 3 * q + n].astype(f32)) for n in range(3)]
+        flags = [jnp.full((1, 128), survive[0, 0, 3 * block_at(q) + n].astype(f32)) for n in range(3)]
         return jnp.concatenate(flags, axis=1).astype(jnp.bfloat16)
 
     def sort(q):
@@ -211,13 +217,6 @@
     def place(p, q, h):
         return (p // 2) * 4 + q // 2, (2 * (p % 2) + h - me1 + 4) % 4
 
-    def each(k, body):
-        @pl.loop(0, k + 1)
-        def _(j):
-            @pl.when((j // 2 + k) % 2 == c)
-            def _():
-                body(j, k)
-
     def tile1(role, i):
         return rcopy(s1.at[role - 1, i], r1.at[3 - role, i], q1s.at[role - 1, i], q1r.at[3 - role, i], ring1(role))
 
@@ -237,22 +236,25 @@
         tables1(k, pl.ds(0, 1), norm)
 
     def compute(k):
-        def body(p, q):
-            tile = jnp.dot(ft[p], fb[q], preferred_element_type=f32)
-            for h in range(2):
-                i, role = place(p, q, h)
-                part = tile[h * TR:(h + 1) * TR]
-
-                @pl.when(role == 0)
-                def _():
-                    kbuf[i] = part
-
-                @pl.when(role > 0)
-                def _():
-                    s1[role - 1, i] = enc1(part, 0, h, p, q)
-                    tile1(role, i).start()
-
-        each(k, body)
+        @pl.loop(0, k // 2 + 1)
+        def _(a):
+            @pl.when((a + k) % 2 == c)
+            def _():
+                both = ft[pl.ds(2 * a, 2)].reshape(2 * CH, 2 * CH)
+                tile = jnp.dot(both, fb[k], preferred_element_type=f32)
+                for n in range(4):
+                    p, h = 2 * a + n // 2, n % 2
+                    i, role = place(p, k, h)
+                    part = tile[n * TR:(n + 1) * TR]
+
+                    @pl.when(jnp.logical_and(role == 0, p <= k))
+                    def _():
+                        kbuf[i] = part
+
+                    @pl.when(jnp.logical_and(role > 0, p <= k))
+                    def _():
+                        s1[role - 1, i] = enc1(part, 0, h, p, k)
+                        tile1(role, i).start()
 
     def norms(k):
         for o in range(1, 4):
@@ -272,15 +274,11 @@
         def _():
             compute(k - 1)
 
-        @pl.when(k > 3)
-        def _():
-            norms(k - 4)
-
         pair(k)
 
     compute(NCH - 1)
 
-    @pl.loop(NCH - 4, NCH)
+    @pl.loop(0, NCH)
     def _(k):
         norms(k)
 
@@ -322,13 +320,13 @@
     tables(4, d2)
 
     def last(m, h, p, q):
-        return rcopy(s3.at[m], r3.at[z], q3s.at[m], q3r.at[z], (q, 2 * p + h))
+        return rcopy(s3.at[m], r3.at[z], q3s.at[m], q3r.at[z], (block_at(q), 2 * block_at(p) + h))
 
     def turned(m, n, h, p, q):
-        return rcopy(s4.at[m, n], r4.at[h, z], q4s.at[m, n], q4r.at[h, z], (p, 2 * q + n))
-
-    def this(a, o):
-        return jnp.logical_and(aux == a, orb == o)
+        return rcopy(s4.at[m, n], r4.at[h, z], q4s.at[m, n], q4r.at[h, z], (block_at(p), 2 * block_at(q) + n))
+
+    def here(q, p, h):
+        return jnp.logical_and(aux == block_at(q), orb == 2 * block_at(p) + h)
 
     @pl.loop(0, 4)
     def _(b):
@@ -345,11 +343,11 @@
             code = jnp.round(tile * (csi[4, pl.ds(q, 1), :] * rbi[4, h, pl.ds(p, 1), :]))
             full = code.astype(jnp.int32).astype(jnp.int16)
 
-            @pl.when(this(q, 2 * p + h))
+            @pl.when(here(q, p, h))
             def _():
                 r3[z] = full
 
-            @pl.when(jnp.logical_not(this(q, 2 * p + h)))
+            @pl.when(jnp.logical_not(here(q, p, h)))
             def _():
                 s3[m] = full
                 last(m, h, p, q).start()
@@ -360,51 +358,53 @@
                     part = code[:, n * TR:(n + 1) * TR]
                     flat = jnp.concatenate([part[:HR], part[HR:]], axis=1).astype(jnp.int32).astype(jnp.int16)
 
-                    @pl.when(this(p, 2 * q + n))
+                    @pl.when(here(p, q, n))
                     def _():
                         r4[h, z] = flat
 
-                    @pl.when(jnp.logical_not(this(p, 2 * q + n)))
+                    @pl.when(jnp.logical_not(here(p, q, n)))
                     def _():
                         s4[m, n] = flat
                         turned(m, n, h, p, q).start()
 
     def other(p, q, h, level):
         src, core = source(p, q, h)
-        return jnp.logical_not(this(2 * level + core, src))
-
-    @pl.when(aux >= pr)
+        return jnp.logical_not(jnp.logical_and(aux == 2 * level + core, orb == src))
+
+    ta, tp = turn_of(aux), turn_of(pr)
+
+    @pl.when(ta >= tp)
     def _():
         h = orb % 2
         for o in range(4):
             up = (z + o) % 4
 
-            @pl.when(other(pr, aux, h, up))
+            @pl.when(other(tp, ta, h, up))
             def _():
                 rcopy(s3.at[0], r3.at[up], q3s.at[0], q3r.at[up], (sib, orb)).wait_recv()
-        tile = dec(r3[z], 4, h, pr, aux)
-        for o in range(1, 4):
-            tile = tile + dec(r3[(z + o) % 4], 4 + o, h, pr, aux)
+        tile = dec(r3[z], 4, h, tp, ta)
+        for o in range(1, 4):
+            tile = tile + dec(r3[(z + o) % 4], 4 + o, h, tp, ta)
         out[...] = tile
 
-    @pl.when(aux < pr)
+    @pl.when(ta < tp)
     def _():
         n = orb % 2
         for h in range(2):
             for o in range(4):
                 up = (z + o) % 4
 
-                @pl.when(other(aux, pr, h, up))
+                @pl.when(other(ta, tp, h, up))
                 def _():
                     rcopy(s4.at[0, 0], r4.at[h, up], q4s.at[0, 0], q4r.at[h, up], (sib, orb)).wait_recv()
         wide = []
         for h in range(2):
             flat = jnp.zeros((HR, CH), f32)
             for o in range(4):
-                sc = cs[4 + o, pl.ds(pr, 1), :]
+                sc = cs[4 + o, pl.ds(tp, 1), :]
                 low = jnp.concatenate([sc[:, :TR], sc[:, :TR]], axis=1)
                 high = jnp.concatenate([sc[:, TR:], sc[:, TR:]], axis=1)
-                sc = jnp.where(n == 0, low, high) * rb[4 + o, h, pl.ds(aux, 1), :]
+                sc = jnp.where(n == 0, low, high) * rb[4 + o, h, pl.ds(ta, 1), :]
                 flat = flat + r4[h, (z + o) % 4].astype(jnp.int32).astype(f32) * sc
             wide.append(jnp.concatenate([flat[:, :TR], flat[:, TR:]], axis=0).T)
         out[...] = jnp.concatenate(wide, axis=1)
@@ -441,12 +441,12 @@
     def _(m):
         h, p, q, ok = where(me1, slot(me2, m))
 
-        @pl.when(jnp.logical_and(ok, jnp.logical_not(this(q, 2 * p + h))))
+        @pl.when(jnp.logical_and(ok, jnp.logical_not(here(q, p, h))))
         def _():
             last(m, h, p, q).wait_send()
 
         for n in range(2):
-            @pl.when(jnp.logical_and(jnp.logical_and(ok, q > p), jnp.logical_not(this(p, 2 * q + n))))
+            @pl.when(jnp.logical_and(jnp.logical_and(ok, q > p), jnp.logical_not(here(p, q, n))))
             def _():
                 turned(m, n, h, p, q).wait_send()
 

time: 86.7 us -> 93.8 us (1.082)
  the two profiles are of different devices: /device:TPU:4 before, /device:TPU:31 now
where the time goes in v9:
time: 93.8 us; the launch traced here: 93.6 us
  Pallas kernels  91.9 us (98%)
  local copies, waits for them, and re-layouts  1.69 us (2%)
    pallas_call x1, Pallas kernels, shards(): pl.pallas_call(kernel, out_shape=jax.ShapeDtypeStruct((TR, CH), f32), in_...  91.9 us

profile of v9, /device:TPU:31, one launch (start us, length us, event | category | flops | bytes accessed | tf_op | source)
XLA Modules:
  0.0 93.6 jit_solution(17252977916561858707)
XLA Ops:
  0.0 91.9 %shard_map.37 = f32[192,384]{1,0:T(8,128)} custom-call(bf16[384,3072]{1,0:T(8,128)(2,1)} %bitcast.1, s32[1,1,24]{2,1,0:T(1,128)} %survive.1, bf16[16,128]{1,0:T(8,128)(2,1)} %metric.1), custom_call_target="tpu_custom_call" | custom-call | tf_op jit(solution)/shard_map/pallas_call | solution.py:473
  91.9 1.7 %copy.5 = f32[192,384]{1,0:T(8,128)} copy(f32[192,384]{1,0:T(8,128)} %shard_map.37) | data formatting | bytes 589824

commit v10 on v8

--- a/solution.py
+++ b/solution.py
@@ -10,6 +10,7 @@
 NCH = 8
 TR = 192
 HR = 96
+LAG = 2
 TOP = 32700.0
 TINY = 1e-36
 ORDER = ((2, 0), (2, 1), (1, 0), (3, 0), (1, 1), (3, 1), (0, 1))
@@ -42,8 +43,8 @@
 
 
 def kernel(half, survive, metric, out, block, perm, whole, snd, rcv, m3, fb, ft, dvr, dv, cs1, csi1, rb1, rbi1, cs, csi, rb, rbi,
-           kbuf, s1, r1, s2, r2, s3, r3, s4, r4,
-           lds, p1s, p1r, ks, kr, fs, fr, d1s, d1r, ds_, dr, q1s, q1r, q2s, q2r, q3s, q3r, q4s, q4r):
+           kbuf, s1f, r1f, s1n, r1n, s2, r2, s3, r3, s4, r4,
+           lds, p1s, p1r, ks, kr, fs, fr, d1s, d1r, ds_, dr, q1fs, q1fr, q1ns, q1nr, q2s, q2r, q3s, q3r, q4s, q4r):
     f32 = jnp.float32
     aux = lax.axis_index("aux")
     orb = lax.axis_index("orb")
@@ -211,15 +212,11 @@
     def place(p, q, h):
         return (p // 2) * 4 + q // 2, (2 * (p % 2) + h - me1 + 4) % 4
 
-    def each(k, body):
-        @pl.loop(0, k + 1)
-        def _(j):
-            @pl.when((j // 2 + k) % 2 == c)
-            def _():
-                body(j, k)
-
-    def tile1(role, i):
-        return rcopy(s1.at[role - 1, i], r1.at[3 - role, i], q1s.at[role - 1, i], q1r.at[3 - role, i], ring1(role))
+    def far(i, n):
+        return rcopy(s1f.at[i, pl.ds(n * HR, HR)], r1f.at[n, i], q1fs.at[i, n], q1fr.at[n, i], ring1(1 + 2 * n))
+
+    def near(i, way, dev):
+        return rcopy(s1n.at[way, i], r1n.at[way, i], q1ns.at[way, i], q1nr.at[way, i], dev)
 
     def tile2(role, m):
         return rcopy(s2.at[role - 1, m], r2.at[3 - role, m], q2s.at[role - 1, m], q2r.at[3 - role, m], ring2(role))
@@ -236,21 +233,45 @@
             dcopy(k, o).start()
         tables1(k, pl.ds(0, 1), norm)
 
+    def each(k, body):
+        @pl.loop(0, k + 1)
+        def _(p):
+            @pl.when((p // 2 + k) % 2 == c)
+            def _():
+                body(p)
+
     def compute(k):
-        def body(p, q):
-            tile = jnp.dot(ft[p], fb[q], preferred_element_type=f32)
+        def body(p):
+            tile = jnp.dot(ft[p], fb[k], preferred_element_type=f32)
             for h in range(2):
-                i, role = place(p, q, h)
+                i, role = place(p, k, h)
                 part = tile[h * TR:(h + 1) * TR]
 
-                @pl.when(role == 0)
+                @pl.when(role == 2)
                 def _():
-                    kbuf[i] = part
-
-                @pl.when(role > 0)
+                    s1f[i] = enc1(part, 0, h, p, k)
+                    far(i, 0).start()
+                    far(i, 1).start()
+
+                @pl.when(role != 2)
                 def _():
-                    s1[role - 1, i] = enc1(part, 0, h, p, q)
-                    tile1(role, i).start()
+                    kbuf[(role + 1) // 2, i] = part
+
+        each(k, body)
+
+    def pass_on(k):
+        def body(p):
+            for h in range(2):
+                i, role = place(p, k, h)
+
+                @pl.when(role % 2 == 1)
+                def _():
+                    way = role // 2
+                    rcopy(s1f.at[i, pl.ds(0, HR)], r1f.at[way, i], q1fs.at[i, 0], q1fr.at[way, i], ring1(1)).wait_recv()
+                    rows = pl.ds(pl.multiple_of(way * HR, 32), HR)
+                    kbuf[1 + way, i, rows, :] = kbuf[1 + way, i, rows, :] + dec1(r1f[way, i], 1 + way, h, p, k)
+                    s1n[way, i] = enc1(kbuf[1 + way, i], 3 + way, h, p, k)
+                    near(i, way, ring1(role)).start()
 
         each(k, body)
 
@@ -258,7 +279,8 @@
         for o in range(1, 4):
             rcopy(dvr.at[0, k], dvr.at[o, k], d1s.at[o, k], d1r.at[o, k], ring1(o)).wait_recv()
         d = [dvr[o, k] for o in range(4)]
-        tables1(k, slice(None), jnp.concatenate(d + d, axis=0))
+        terms = [d[0], d[3], d[1], d[0] + d[3], d[0] + d[1], d[3] + d[2], d[1] + d[2], d[0]]
+        tables1(k, slice(None), jnp.concatenate(terms, axis=0))
         dv[4, pl.ds(k, 1), :] = d[0] + d[1] + d[2] + d[3]
 
     @pl.loop(0, NCH)
@@ -272,19 +294,25 @@
         def _():
             compute(k - 1)
 
-        @pl.when(k > 3)
+        @pl.when(k >= LAG)
         def _():
-            norms(k - 4)
+            norms(k - LAG)
+            pass_on(k - LAG)
 
         pair(k)
 
     compute(NCH - 1)
 
-    @pl.loop(NCH - 4, NCH)
+    @pl.loop(NCH - LAG, NCH)
     def _(k):
         norms(k)
 
     gather(1, ring2)
+
+    @pl.loop(NCH - LAG, NCH)
+    def _(k):
+        pass_on(k)
+
 
     d1 = gathered(1, ring2)
     tables(0, d1)
@@ -304,14 +332,13 @@
 
         @pl.when(ok)
         def _():
-            tile = kbuf[i]
-            for o in range(1, 4):
-                rcopy(s1.at[0, i], r1.at[o - 1, i], q1s.at[0, i], q1r.at[o - 1, i], ring1(1)).wait_recv()
-                tile = tile + dec1(r1[o - 1, i], o, h, p, q)
+            near(i, 0, ring1(1)).wait_recv()
+            near(i, 1, ring1(1)).wait_recv()
+            tile = kbuf[0, i] + dec1(r1n[0, i], 5, h, p, q) + dec1(r1n[1, i], 6, h, p, q)
 
             @pl.when(role == 0)
             def _():
-                kbuf[i] = tile
+                kbuf[0, i] = tile
 
             @pl.when(role > 0)
             def _():
@@ -327,8 +354,8 @@
     def turned(m, n, h, p, q):
         return rcopy(s4.at[m, n], r4.at[h, z], q4s.at[m, n], q4r.at[h, z], (p, 2 * q + n))
 
-    def this(a, o):
-        return jnp.logical_and(aux == a, orb == o)
+    def here(q, p, h):
+        return jnp.logical_and(aux == q, orb == 2 * p + h)
 
     @pl.loop(0, 4)
     def _(b):
@@ -338,18 +365,18 @@
 
         @pl.when(ok)
         def _():
-            tile = kbuf[i]
+            tile = kbuf[0, i]
             for n in range(1, 4):
                 rcopy(s2.at[0, m], r2.at[n - 1, m], q2s.at[0, m], q2r.at[n - 1, m], ring2(1)).wait_recv()
                 tile = tile + dec(r2[n - 1, m], n, h, p, q)
             code = jnp.round(tile * (csi[4, pl.ds(q, 1), :] * rbi[4, h, pl.ds(p, 1), :]))
             full = code.astype(jnp.int32).astype(jnp.int16)
 
-            @pl.when(this(q, 2 * p + h))
+            @pl.when(here(q, p, h))
             def _():
                 r3[z] = full
 
-            @pl.when(jnp.logical_not(this(q, 2 * p + h)))
+            @pl.when(jnp.logical_not(here(q, p, h)))
             def _():
                 s3[m] = full
                 last(m, h, p, q).start()
@@ -360,18 +387,18 @@
                     part = code[:, n * TR:(n + 1) * TR]
                     flat = jnp.concatenate([part[:HR], part[HR:]], axis=1).astype(jnp.int32).astype(jnp.int16)
 
-                    @pl.when(this(p, 2 * q + n))
+                    @pl.when(here(p, q, n))
                     def _():
                         r4[h, z] = flat
 
-                    @pl.when(jnp.logical_not(this(p, 2 * q + n)))
+                    @pl.when(jnp.logical_not(here(p, q, n)))
                     def _():
                         s4[m, n] = flat
                         turned(m, n, h, p, q).start()
 
     def other(p, q, h, level):
         src, core = source(p, q, h)
-        return jnp.logical_not(this(2 * level + core, src))
+        return jnp.logical_not(jnp.logical_and(aux == 2 * level + core, orb == src))
 
     @pl.when(aux >= pr)
     def _():
@@ -429,7 +456,11 @@
         def _(i):
             @pl.when(where((me1 + role) % 4, i)[3])
             def _():
-                tile1(role, i).wait_send()
+                if role == 2:
+                    far(i, 0).wait_send()
+                    far(i, 1).wait_send()
+                else:
+                    near(i, role // 2, ring1(1)).wait_send()
 
         @pl.loop(0, 4)
         def _(m):
@@ -441,12 +472,12 @@
     def _(m):
         h, p, q, ok = where(me1, slot(me2, m))
 
-        @pl.when(jnp.logical_and(ok, jnp.logical_not(this(q, 2 * p + h))))
+        @pl.when(jnp.logical_and(ok, jnp.logical_not(here(q, p, h))))
         def _():
             last(m, h, p, q).wait_send()
 
         for n in range(2):
-            @pl.when(jnp.logical_and(jnp.logical_and(ok, q > p), jnp.logical_not(this(p, 2 * q + n))))
+            @pl.when(jnp.logical_and(jnp.logical_and(ok, q > p), jnp.logical_not(here(p, q, n))))
             def _():
                 turned(m, n, h, p, q).wait_send()
 
@@ -462,12 +493,13 @@
         vm((4, NCH, 1, CH), f32), vm((12, 8, CH), f32),
         vm((NCH, 8, CH), f32), vm((NCH, 8, CH), f32), vm((2, NCH, 8, CH), f32), vm((2, NCH, 8, CH), f32),
         vm((8, 8, CH), f32), vm((8, 8, CH), f32), vm((8, 2, 8, CH), f32), vm((8, 2, 8, CH), f32),
-        vm((16, TR, CH), f32), vm((3, 16, TR, CH), i16), vm((3, 16, TR, CH), i16),
+        vm((3, 16, TR, CH), f32),
+        vm((16, TR, CH), i16), vm((2, 16, HR, CH), i16), vm((2, 16, TR, CH), i16), vm((2, 16, TR, CH), i16),
         vm((3, 4, TR, CH), i16), vm((3, 4, TR, CH), i16),
         vm((4, TR, CH), i16), vm((4, TR, CH), i16), vm((4, 2, HR, CH), i16), vm((2, 4, HR, CH), i16),
         dma((NCH,)), dma((NCH, 8)), dma((NCH, 8)), dma((8,)), dma((8,)), dma((NCH,)), dma((NCH,)),
         dma((4, NCH)), dma((4, NCH)), dma((12,)), dma((12,)),
-        dma((3, 16)), dma((3, 16)), dma((3, 4)), dma((3, 4)),
+        dma((16, 2)), dma((2, 16)), dma((2, 16)), dma((2, 16)), dma((3, 4)), dma((3, 4)),
         dma((4,)), dma((4,)), dma((4, 2)), dma((2, 4)),
     ]
     return pl.pallas_call(

time: 86.7 us -> 81.3 us (0.938)
  the two profiles are of different devices: /device:TPU:4 before, /device:TPU:47 now
where the time goes in v10:
time: 81.3 us; the launch traced here: 80.5 us
  Pallas kernels  78.8 us (97%)
  local copies, waits for them, and re-layouts  1.69 us (2%)
    pallas_call x1, Pallas kernels, shards(): pl.pallas_call(kernel, out_shape=jax.ShapeDtypeStruct((TR, CH), f32), in_...  78.8 us
    unnamed x1, local copies, waits for them, and re-layouts  1.69 us

profile of v10, /device:TPU:47, one launch (start us, length us, event | category | flops | bytes accessed | tf_op | source)
XLA Modules:
  0.0 80.5 jit_solution(4311247388671746959)
XLA Ops:
  0.0 78.8 %shard_map.37 = f32[192,384]{1,0:T(8,128)} custom-call(bf16[384,3072]{1,0:T(8,128)(2,1)} %bitcast.1, s32[1,1,24]{2,1,0:T(1,128)} %survive.1, bf16[16,128]{1,0:T(8,128)(2,1)} %metric.1), custom_call_target="tpu_custom_call" | custom-call | tf_op jit(solution)/shard_map/pallas_call | solution.py:505
  78.8 1.7 %copy.5 = f32[192,384]{1,0:T(8,128)} copy(f32[192,384]{1,0:T(8,128)} %shard_map.37) | data formatting | bytes 589824

commit v11 on v10

--- a/solution.py
+++ b/solution.py
@@ -42,32 +42,33 @@
     return jnp.where(a - 3.0 * third(a) == b - 3.0 * third(b), wide, 0.0).astype(bf)
 
 
-def kernel(half, survive, metric, out, block, perm, whole, snd, rcv, m3, fb, ft, dvr, dv, cs1, csi1, rb1, rbi1, cs, csi, rb, rbi,
+def kernel(half, survive, metric, out, block, perm, whole, snd, rcv, m3, fb, ft, dvr, dv, dvx, cs1, csi1, rb1, rbi1, cs, csi, rb, rbi,
            kbuf, s1f, r1f, s1n, r1n, s2, r2, s3, r3, s4, r4,
-           lds, p1s, p1r, ks, kr, fs, fr, d1s, d1r, ds_, dr, q1fs, q1fr, q1ns, q1nr, q2s, q2r, q3s, q3r, q4s, q4r):
+           lds, p1s, p1r, ks, kr, fs, fr, d1s, d1r, ds_, dr, dxs, dxr, q1fs, q1fr, q1ns, q1nr, q2s, q2r, q3s, q3r, q4s, q4r):
     f32 = jnp.float32
     aux = lax.axis_index("aux")
     orb = lax.axis_index("orb")
     z, c = aux // 2, aux % 2
     x, y = orb // 4, orb % 4
     me1 = x * (1 - c) + y * c
-    me2 = y * (1 - c) + x * c
+    me2 = z
+    me3 = y * (1 - c) + x * c
     sib = 2 * z + 1 - c
 
     def row_of(t, u):
         return t * (4 - 3 * c) + u * (1 + 3 * c)
 
     def ring1(o):
-        return (aux, row_of((me1 + o) % 4, me2))
+        return (aux, row_of((me1 + o) % 4, me3))
 
     def ring2(o):
-        return (aux, row_of(me1, (me2 + o) % 4))
+        return (2 * ((z + o) % 4) + c, orb)
+
+    def line3(o):
+        return (aux, row_of(me1, (me3 + o) % 4))
 
     def cross(o):
-        return (sib, row_of(me1, (me2 + o) % 4))
-
-    def zdev(o, core):
-        return (2 * ((z + o) % 4) + core, orb)
+        return (sib, row_of(me1, (me3 + o) % 4))
 
     pr = orb // 2
     def cut(q):
@@ -84,7 +85,7 @@
         pl.semaphore_signal(bar, inc=1, device_id=((aux + o) % 8, orb), device_id_type=MESH)
     for o in range(1, 4):
         pl.semaphore_signal(bar, inc=1, device_id=ring1(o), device_id_type=MESH)
-        pl.semaphore_signal(bar, inc=1, device_id=ring2(o), device_id_type=MESH)
+        pl.semaphore_signal(bar, inc=1, device_id=line3(o), device_id_type=MESH)
         pl.semaphore_signal(bar, inc=1, device_id=cross(o), device_id_type=MESH)
 
     def rcopy(src, dst, ss, rs, dev):
@@ -204,10 +205,10 @@
     def slot(u, m):
         return m * 4 + (u - m + 4) % 4
 
-    def source(p, q, h):
+    def source(p, q, h, v):
         core = (p // 2 + q) % 2
         t, u = 2 * (p % 2) + h, (p // 2 + q // 2) % 4
-        return t * (4 - 3 * core) + u * (1 + 3 * core), core
+        return 2 * u + core, t * (4 - 3 * core) + v * (1 + 3 * core)
 
     def place(p, q, h):
         return (p // 2) * 4 + q // 2, (2 * (p % 2) + h - me1 + 4) % 4
@@ -318,10 +319,7 @@
     tables(0, d1)
     dv[8] = d1[0] + d1[1] + d1[2] + d1[3]
 
-    def zline(o):
-        return zdev(o, c)
-
-    gather(2, zline)
+    gather(2, line3)
     @pl.loop(0, 16)
     def _(n):
         b = n // 4
@@ -345,14 +343,19 @@
                 s2[role - 1, a] = enc(tile, 0, h, p, q)
                 tile2(role, a).start()
 
-    d2 = gathered(2, zline)
+    d2 = gathered(2, line3)
     tables(4, d2)
 
+    def swap():
+        return rcopy(dv.at[pl.ds(8, 4)], dvx, dxs, dxr, (sib, orb))
+
+    swap().start()
+
     def last(m, h, p, q):
-        return rcopy(s3.at[m], r3.at[z], q3s.at[m], q3r.at[z], (q, 2 * p + h))
+        return rcopy(s3.at[m], r3.at[me3], q3s.at[m], q3r.at[me3], (q, 2 * p + h))
 
     def turned(m, n, h, p, q):
-        return rcopy(s4.at[m, n], r4.at[h, z], q4s.at[m, n], q4r.at[h, z], (p, 2 * q + n))
+        return rcopy(s4.at[m, n], r4.at[h, me3], q4s.at[m, n], q4r.at[h, me3], (p, 2 * q + n))
 
     def here(q, p, h):
         return jnp.logical_and(aux == q, orb == 2 * p + h)
@@ -374,7 +377,7 @@
 
             @pl.when(here(q, p, h))
             def _():
-                r3[z] = full
+                r3[me3] = full
 
             @pl.when(jnp.logical_not(here(q, p, h)))
             def _():
@@ -389,37 +392,46 @@
 
                     @pl.when(here(p, q, n))
                     def _():
-                        r4[h, z] = flat
+                        r4[h, me3] = flat
 
                     @pl.when(jnp.logical_not(here(p, q, n)))
                     def _():
                         s4[m, n] = flat
                         turned(m, n, h, p, q).start()
 
-    def other(p, q, h, level):
-        src, core = source(p, q, h)
-        return jnp.logical_not(jnp.logical_and(aux == 2 * level + core, orb == src))
+    def other(p, q, h, v):
+        a, o = source(p, q, h, v)
+        return jnp.logical_not(jnp.logical_and(aux == a, orb == o))
+
+    swap().wait_recv()
+    tables(8, [dvx[o] for o in range(4)])
+
+    def family(p, q):
+        apart = (p // 2 + q + c) % 2
+        return 4 + 4 * apart, me3 + apart * (me1 - me3)
 
     @pl.when(aux >= pr)
     def _():
         h = orb % 2
+        first, v = family(pr, aux)
         for o in range(4):
-            up = (z + o) % 4
+            up = (v + o) % 4
 
             @pl.when(other(pr, aux, h, up))
             def _():
                 rcopy(s3.at[0], r3.at[up], q3s.at[0], q3r.at[up], (sib, orb)).wait_recv()
-        tile = dec(r3[z], 4, h, pr, aux)
-        for o in range(1, 4):
-            tile = tile + dec(r3[(z + o) % 4], 4 + o, h, pr, aux)
+        tile = dec(r3[v], first, h, pr, aux)
+        for o in range(1, 4):
+            tile = tile + dec(r3[(v + o) % 4], first + o, h, pr, aux)
         out[...] = tile
 
     @pl.when(aux < pr)
     def _():
         n = orb % 2
+        first, v = family(aux, pr)
         for h in range(2):
             for o in range(4):
-                up = (z + o) % 4
+                up = (v + o) % 4
 
                 @pl.when(other(aux, pr, h, up))
                 def _():
@@ -428,14 +440,15 @@
         for h in range(2):
             flat = jnp.zeros((HR, CH), f32)
             for o in range(4):
-                sc = cs[4 + o, pl.ds(pr, 1), :]
+                sc = cs[first + o, pl.ds(pr, 1), :]
                 low = jnp.concatenate([sc[:, :TR], sc[:, :TR]], axis=1)
                 high = jnp.concatenate([sc[:, TR:], sc[:, TR:]], axis=1)
-                sc = jnp.where(n == 0, low, high) * rb[4 + o, h, pl.ds(aux, 1), :]
-                flat = flat + r4[h, (z + o) % 4].astype(jnp.int32).astype(f32) * sc
+                sc = jnp.where(n == 0, low, high) * rb[first + o, h, pl.ds(aux, 1), :]
+                flat = flat + r4[h, (v + o) % 4].astype(jnp.int32).astype(f32) * sc
             wide.append(jnp.concatenate([flat[:, :TR], flat[:, TR:]], axis=0).T)
         out[...] = jnp.concatenate(wide, axis=1)
 
+    swap().wait_send()
     for o in range(1, 8):
         mcopy(o).wait_send()
 
@@ -447,7 +460,7 @@
         for o in range(1, 4):
             dcopy(q, o).wait_send()
 
-    for level, dev in ((1, ring2), (2, zline)):
+    for level, dev in ((1, ring2), (2, line3)):
         for o in range(1, 4):
             rcopy(dv.at[4 * level], dv.at[4 * level], ds_.at[4 * level + o], dr.at[4 * level], dev(o)).wait_send()
 
@@ -490,15 +503,15 @@
         vm((NCH, CH, CH), bf), vm((CH, CH), bf), vm((128, 128), bf),
         vm((NCH, CH, CH), bf), vm((NCH, CH, CH), bf), vm((CH, CH), bf),
         vm((NCH, 2 * CH, CH), bf), vm((NCH, CH, 2 * CH), bf),
-        vm((4, NCH, 1, CH), f32), vm((12, 8, CH), f32),
+        vm((4, NCH, 1, CH), f32), vm((12, 8, CH), f32), vm((4, 8, CH), f32),
         vm((NCH, 8, CH), f32), vm((NCH, 8, CH), f32), vm((2, NCH, 8, CH), f32), vm((2, NCH, 8, CH), f32),
-        vm((8, 8, CH), f32), vm((8, 8, CH), f32), vm((8, 2, 8, CH), f32), vm((8, 2, 8, CH), f32),
+        vm((12, 8, CH), f32), vm((12, 8, CH), f32), vm((12, 2, 8, CH), f32), vm((12, 2, 8, CH), f32),
         vm((3, 16, TR, CH), f32),
         vm((16, TR, CH), i16), vm((2, 16, HR, CH), i16), vm((2, 16, TR, CH), i16), vm((2, 16, TR, CH), i16),
         vm((3, 4, TR, CH), i16), vm((3, 4, TR, CH), i16),
         vm((4, TR, CH), i16), vm((4, TR, CH), i16), vm((4, 2, HR, CH), i16), vm((2, 4, HR, CH), i16),
         dma((NCH,)), dma((NCH, 8)), dma((NCH, 8)), dma((8,)), dma((8,)), dma((NCH,)), dma((NCH,)),
-        dma((4, NCH)), dma((4, NCH)), dma((12,)), dma((12,)),
+        dma((4, NCH)), dma((4, NCH)), dma((12,)), dma((12,)), dma, dma,
         dma((16, 2)), dma((2, 16)), dma((2, 16)), dma((2, 16)), dma((3, 4)), dma((3, 4)),
         dma((4,)), dma((4,)), dma((4, 2)), dma((2, 4)),
     ]

time: 81.3 us -> 97.9 us (1.20)
  the two profiles are of different devices: /device:TPU:47 before, /device:TPU:14 now
where the time goes in v11:
time: 97.9 us; the launch traced here: 97.7 us
  Pallas kernels  96 us (98%)
  local copies, waits for them, and re-layouts  1.69 us (2%)
    pallas_call x1, Pallas kernels, shards(): pl.pallas_call(kernel, out_shape=jax.ShapeDtypeStruct((TR, CH), f32), in_...  96 us

profile of v11, /device:TPU:14, one launch (start us, length us, event | category | flops | bytes accessed | tf_op | source)
XLA Modules:
  0.0 97.7 jit_solution(355390208593434476)
XLA Ops:
  0.0 96.0 %shard_map.37 = f32[192,384]{1,0:T(8,128)} custom-call(bf16[384,3072]{1,0:T(8,128)(2,1)} %bitcast.1, s32[1,1,24]{2,1,0:T(1,128)} %survive.1, bf16[16,128]{1,0:T(8,128)(2,1)} %metric.1), custom_call_target="tpu_custom_call" | custom-call | tf_op jit(solution)/shard_map/pallas_call | solution.py:518
  96.0 1.7 %copy.5 = f32[192,384]{1,0:T(8,128)} copy(f32[192,384]{1,0:T(8,128)} %shard_map.37) | data formatting | bytes 589824

commit v12 on v10

--- a/solution.py
+++ b/solution.py
@@ -13,7 +13,7 @@
 LAG = 2
 TOP = 32700.0
 TINY = 1e-36
-ORDER = ((2, 0), (2, 1), (1, 0), (3, 0), (1, 1), (3, 1), (0, 1))
+ORDER = ((0, 1), (2, 0), (1, 0), (3, 0), (2, 1), (1, 1), (3, 1))
 
 
 def third(n):
@@ -303,15 +303,11 @@
 
     compute(NCH - 1)
 
-    @pl.loop(NCH - LAG, NCH)
-    def _(k):
-        norms(k)
-
+    norms(NCH - 2)
+    pass_on(NCH - 2)
+    norms(NCH - 1)
     gather(1, ring2)
-
-    @pl.loop(NCH - LAG, NCH)
-    def _(k):
-        pass_on(k)
+    pass_on(NCH - 1)
 
 
     d1 = gathered(1, ring2)

time: 81.3 us -> 80.3 us (0.988)
  no operation moved by 1% of the time
where the time goes in v12:
time: 80.3 us; the launch traced here: 80.1 us
  Pallas kernels  78.4 us (98%)
  local copies, waits for them, and re-layouts  1.69 us (2%)
    pallas_call x1, Pallas kernels, shards(): pl.pallas_call(kernel, out_shape=jax.ShapeDtypeStruct((TR, CH), f32), in_...  78.4 us
    unnamed x1, local copies, waits for them, and re-layouts  1.69 us

profile of v12, /device:TPU:47, one launch (start us, length us, event | category | flops | bytes accessed | tf_op | source)
XLA Modules:
  0.0 80.1 jit_solution(6823671029529813919)
XLA Ops:
  0.0 78.4 %shard_map.37 = f32[192,384]{1,0:T(8,128)} custom-call(bf16[384,3072]{1,0:T(8,128)(2,1)} %bitcast.1, s32[1,1,24]{2,1,0:T(1,128)} %survive.1, bf16[16,128]{1,0:T(8,128)(2,1)} %metric.1), custom_call_target="tpu_custom_call" | custom-call | tf_op jit(solution)/shard_map/pallas_call | solution.py:501
  78.4 1.7 %copy.5 = f32[192,384]{1,0:T(8,128)} copy(f32[192,384]{1,0:T(8,128)} %shard_map.37) | data formatting | bytes 589824

commit v13 on v12

--- a/solution.py
+++ b/solution.py
@@ -241,23 +241,26 @@
                 body(p)
 
     def compute(k):
-        def body(p):
-            tile = jnp.dot(ft[p], fb[k], preferred_element_type=f32)
-            for h in range(2):
-                i, role = place(p, k, h)
-                part = tile[h * TR:(h + 1) * TR]
-
-                @pl.when(role == 2)
-                def _():
-                    s1f[i] = enc1(part, 0, h, p, k)
-                    far(i, 0).start()
-                    far(i, 1).start()
-
-                @pl.when(role != 2)
-                def _():
-                    kbuf[(role + 1) // 2, i] = part
-
-        each(k, body)
+        @pl.loop(0, k // 2 + 1)
+        def _(a):
+            @pl.when((a + k) % 2 == c)
+            def _():
+                both = ft[pl.ds(2 * a, 2)].reshape(2 * CH, 2 * CH)
+                tile = jnp.dot(both, fb[k], preferred_element_type=f32)
+                for n in range(4):
+                    p, h = 2 * a + n // 2, n % 2
+                    i, role = place(p, k, h)
+                    part = tile[n * TR:(n + 1) * TR]
+
+                    @pl.when(jnp.logical_and(role == 2, p <= k))
+                    def _():
+                        s1f[i] = enc1(part, 0, h, p, k)
+                        far(i, 0).start()
+                        far(i, 1).start()
+
+                    @pl.when(jnp.logical_and(role != 2, p <= k))
+                    def _():
+                        kbuf[(role + 1) // 2, i] = part
 
     def pass_on(k):
         def body(p):

time: 80.3 us -> 80.5 us (level)
  no operation moved by 1% of the time
where the time goes in v13:
time: 80.5 us; the launch traced here: 80.4 us
  Pallas kernels  78.6 us (98%)
  local copies, waits for them, and re-layouts  1.69 us (2%)
    pallas_call x1, Pallas kernels, shards(): pl.pallas_call(kernel, out_shape=jax.ShapeDtypeStruct((TR, CH), f32), in_...  78.6 us
    unnamed x1, local copies, waits for them, and re-layouts  1.69 us

profile of v13, /device:TPU:47, one launch (start us, length us, event | category | flops | bytes accessed | tf_op | source)
XLA Modules:
  0.0 80.4 jit_solution(17000603102702208128)
XLA Ops:
  0.0 78.6 %shard_map.37 = f32[192,384]{1,0:T(8,128)} custom-call(bf16[384,3072]{1,0:T(8,128)(2,1)} %bitcast.1, s32[1,1,24]{2,1,0:T(1,128)} %survive.1, bf16[16,128]{1,0:T(8,128)(2,1)} %metric.1), custom_call_target="tpu_custom_call" | custom-call | tf_op jit(solution)/shard_map/pallas_call | solution.py:504
  78.7 1.7 %copy.5 = f32[192,384]{1,0:T(8,128)} copy(f32[192,384]{1,0:T(8,128)} %shard_map.37) | data formatting | bytes 589824

commit v14 on v13

--- a/solution.py
+++ b/solution.py
@@ -314,13 +314,13 @@
 
 
     d1 = gathered(1, ring2)
-    tables(0, d1)
     dv[8] = d1[0] + d1[1] + d1[2] + d1[3]
 
     def zline(o):
         return zdev(o, c)
 
     gather(2, zline)
+    tables(0, d1)
     @pl.loop(0, 16)
     def _(n):
         b = n // 4

time: 80.5 us -> 80.5 us (level)
  no operation moved by 1% of the time
where the time goes in v14:
time: 80.5 us; the launch traced here: 80.4 us
  Pallas kernels  78.6 us (98%)
  local copies, waits for them, and re-layouts  1.69 us (2%)
    pallas_call x1, Pallas kernels, shards(): pl.pallas_call(kernel, out_shape=jax.ShapeDtypeStruct((TR, CH), f32), in_...  78.6 us
    unnamed x1, local copies, waits for them, and re-layouts  1.69 us

profile of v14, /device:TPU:47, one launch (start us, length us, event | category | flops | bytes accessed | tf_op | source)
XLA Modules:
  0.0 80.4 jit_solution(7743287203569578519)
XLA Ops:
  0.0 78.6 %shard_map.37 = f32[192,384]{1,0:T(8,128)} custom-call(bf16[384,3072]{1,0:T(8,128)(2,1)} %bitcast.1, s32[1,1,24]{2,1,0:T(1,128)} %survive.1, bf16[16,128]{1,0:T(8,128)(2,1)} %metric.1), custom_call_target="tpu_custom_call" | custom-call | tf_op jit(solution)/shard_map/pallas_call | solution.py:504
  78.7 1.7 %copy.5 = f32[192,384]{1,0:T(8,128)} copy(f32[192,384]{1,0:T(8,128)} %shard_map.37) | data formatting | bytes 589824
